TPU v7x, 512 devices: a whole 4x8x8 slice. The times are simulated.
512 devices in a mesh: section: 8 (over z), sht: 64 (over x, y, core).
Axes of the slice: x: 4, y: 8, z: 8, core: 2. Of those that a mesh axis runs over, the one named last changes fastest.
Arguments:
- analysis: bfloat16 [128, 256, 192], P('sht', None, 'section'), may hold values from -6 to 6
- perturbations: bfloat16 [6, 128, 256, 192], P(None, 'sht', None, 'section'), may hold values from -6 to 6
- gain_first: float32 [8, 192], P('section'), may hold values from 0.1 to 1.9
- spectral_gain: float32 [8, 2, 24576], P('section'), may hold values from -6 to 6
- skip_weight: bfloat16 [8, 192, 192], P('section'), may hold values from -0.4375 to 0.4375
- gain_second: float32 [8, 192], P('section'), may hold values from 0.1 to 1.9
- mlp_in: bfloat16 [8, 192, 384], P('section'), may hold values from -0.4375 to 0.4375
- mlp_out: bfloat16 [8, 192, 384], P('section'), may hold values from -0.3125 to 0.3125
Outputs:
- block_outputs: bfloat16 [8, 6, 128, 49152], P('section', None, 'sht')
All inputs are finite; a program needn't handle non-finite values.
Results may differ from a plain program's by a relative error of at most 0.025.
Values may be sent and summed in bfloat16 or wider, within the bound.
A program may use at most 64 MiB of HBM per device.

v0:
```python
import math

import jax
import jax.numpy as jnp
from jax import lax
from jax.sharding import PartitionSpec as P

C = 192
NLAT = 128
NLON = 256
LMAX = 128
MMAX = 128


def from_everyone(shard, axis):
    copies = jnp.broadcast_to(shard, (lax.axis_size(axis), *shard.shape))
    return lax.all_to_all(copies, axis, split_axis=0, concat_axis=0, tiled=True)


def in_order(tiles, dim):
    lengths = list(tiles.shape[1:])
    lengths[dim] *= tiles.shape[0]
    return jnp.moveaxis(tiles, 0, dim).reshape(lengths)


def gather_directly(shard, axis, dim):
    tiles = from_everyone(shard, axis)
    return in_order(tiles, dim)


def shifted_2(value, axis, steps):
    count = lax.axis_size(axis)
    first, last = (max(0, -steps), min(count, count - steps))
    return lax.ppermute(value, axis, [(source, source + steps) for source in range(first, last)])


def legendre_table(nlat, lmax, mmax, nlon, m_first, m_count):
    latitudes = jnp.arange(nlat, dtype=jnp.float32)
    colatitude = math.pi * (latitudes + 0.5) / nlat
    cosine = jnp.cos(colatitude)
    sine = jnp.sin(colatitude)
    orders = jnp.arange(1, mmax, dtype=jnp.float32)
    factors = jnp.cumsum(0.5 * jnp.log((2.0 * orders + 1.0) / (2.0 * orders)))
    log_diag = jnp.concatenate([jnp.zeros((1,), jnp.float32), factors])
    m_index = m_first + jnp.arange(m_count, dtype=jnp.int32)
    picked = jnp.sum(
        jnp.where(
            m_index[:, None] == jnp.arange(mmax, dtype=jnp.int32)[None, :], log_diag[None, :], 0.0
        ),
        axis=1,
    )
    m_float = m_index.astype(jnp.float32)
    diagonal = jnp.exp(picked[None, :] + m_float[None, :] * jnp.log(sine)[:, None]) * math.sqrt(
        0.25 / math.pi
    )
    cos_col = cosine[:, None]

    def advance(carry, degree):
        latest, earlier = carry
        degree_float = degree.astype(jnp.float32)
        lower = jnp.sqrt(
            (4.0 * degree_float * degree_float - 1.0)
            / jnp.maximum(degree_float * degree_float - m_float * m_float, 1.0)
        )
        shifted = degree_float - 1.0
        upper = jnp.sqrt(
            jnp.maximum(shifted * shifted - m_float * m_float, 0.0)
            / jnp.maximum(4.0 * shifted * shifted - 1.0, 1.0)
        )
        recurred = lower[None, :] * (cos_col * latest - upper[None, :] * earlier)
        first_step = jnp.sqrt(2.0 * m_float + 3.0)[None, :] * cos_col * diagonal
        current = jnp.where(
            degree == m_index[None, :],
            diagonal,
            jnp.where(
                degree == m_index[None, :] + 1,
                first_step,
                jnp.where(degree > m_index[None, :] + 1, recurred, 0.0),
            ),
        )
        return ((current, latest), current)

    initial = jnp.zeros((nlat, m_count), jnp.float32)
    _, stacked = lax.scan(advance, (initial, initial), jnp.arange(lmax, dtype=jnp.int32), unroll=8)
    legendre = jnp.transpose(stacked, (1, 0, 2))
    weights = sine * (2.0 * math.pi / nlon) * (math.pi / nlat)
    return (legendre, weights)


def fourier_tables(nlon, mmax):
    samples = jnp.arange(nlon, dtype=jnp.int32)
    orders = jnp.arange(mmax, dtype=jnp.int32)
    phase = (samples[:, None] * orders[None, :] % nlon).astype(jnp.float32) * (2.0 * math.pi / nlon)
    cosines = jnp.cos(phase)
    sines = jnp.sin(phase)
    forward = jnp.stack([cosines, -sines], axis=1).astype(jnp.bfloat16)
    factor = jnp.where(orders == 0, 1.0, 2.0).astype(jnp.float32)
    inverse = jnp.stack([cosines.T * factor[:, None], -sines.T * factor[:, None]], axis=0).astype(
        jnp.bfloat16
    )
    return (forward, inverse)


def layer_norm(values, gain_vector):
    average = jnp.mean(values, axis=-1, keepdims=True)
    centred = values - average
    variance = jnp.mean(centred * centred, axis=-1, keepdims=True)
    return centred * lax.rsqrt(variance + 1e-05) * gain_vector


def apply_gain(coeffs, gain_table):
    real_part = coeffs[:, :, :, 0]
    imag_part = coeffs[:, :, :, 1]
    gain_real = gain_table[0][None, :, None, :]
    gain_imag = gain_table[1][None, :, None, :]
    return jnp.stack(
        [
            real_part * gain_real - imag_part * gain_imag,
            real_part * gain_imag + imag_part * gain_real,
        ],
        axis=3,
    )


def recenter(analysis, perturbations):
    pert_wide = perturbations.astype(jnp.float32)
    average = jnp.mean(pert_wide, axis=0, keepdims=True)
    return (analysis.astype(jnp.float32)[None] + pert_wide - average).astype(jnp.bfloat16)


def project_out(hidden, out_matrix):
    return lax.dot_general(
        hidden, out_matrix, (((1,), (1,)), ((), ())), preferred_element_type=jnp.float32
    )


def per_device(
    analysis, perturbations, gain_first, spectral_gain, skip_weight, gain_second, mlp_in, mlp_out
):
    section_index = lax.axis_index("section")
    section_count = lax.axis_size("section")
    member_count = perturbations.shape[0]
    stacked = jnp.concatenate([analysis[None], perturbations], axis=0)
    gathered = gather_directly(stacked, "section", 3)
    members = recenter(gathered[0], gathered[1:])
    forward, inverse = fourier_tables(NLON, MMAX)
    full_gain = spectral_gain[0].reshape(2, LMAX, C)
    m_count = MMAX // lax.axis_size("sht")
    legendre, weights = legendre_table(
        NLAT, LMAX, MMAX, NLON, lax.axis_index("sht") * m_count, m_count
    )
    weighted = (legendre * weights[:, None, None]).astype(jnp.bfloat16)
    plain_table = legendre.astype(jnp.bfloat16)

    def spectral(normed):
        batch_rows = normed.shape[0]
        lat_rows = normed.shape[1]
        spectrum = jnp.einsum(
            "bjkc,kpm->bjmpc", normed, forward, preferred_element_type=jnp.float32
        ).astype(jnp.bfloat16)
        spectrum = spectrum.reshape(batch_rows, lat_rows, MMAX, 2 * C)
        exchanged = lax.all_to_all(spectrum, "sht", split_axis=2, concat_axis=1, tiled=True)
        item_count = exchanged.shape[0]
        coeffs = jnp.einsum(
            "jlm,bjmq->blmq", weighted, exchanged, preferred_element_type=jnp.float32
        )
        coeffs = coeffs.reshape(item_count, LMAX, m_count, 2, C)
        filtered = (
            apply_gain(coeffs, full_gain)
            .astype(jnp.bfloat16)
            .reshape(item_count, LMAX, m_count, 2 * C)
        )
        returned = jnp.einsum(
            "jlm,blmq->bjmq", plain_table, filtered, preferred_element_type=jnp.float32
        ).astype(jnp.bfloat16)
        returned = lax.all_to_all(returned, "sht", split_axis=1, concat_axis=2, tiled=True)
        returned = returned.reshape(batch_rows, lat_rows, MMAX, 2, C)
        return jnp.einsum("bjmpc,pmk->bjkc", returned, inverse, preferred_element_type=jnp.float32)

    def sfno_block(current_state):
        state_wide = current_state.astype(jnp.float32)
        channels = current_state.shape[-1]
        normed = layer_norm(state_wide, gain_first[0]).astype(jnp.bfloat16)
        spatial = spectral(normed)
        skipped = jnp.dot(
            normed.reshape(-1, channels), skip_weight[0], preferred_element_type=jnp.float32
        ).reshape(spatial.shape)
        activated = jax.nn.gelu(spatial + skipped, approximate=False)
        second = layer_norm(activated, gain_second[0]).astype(jnp.bfloat16)
        hidden = jax.nn.gelu(
            jnp.dot(second.reshape(-1, channels), mlp_in[0], preferred_element_type=jnp.float32),
            approximate=False,
        ).astype(jnp.bfloat16)
        update = project_out(hidden, mlp_out[0]).reshape(spatial.shape)
        return (state_wide + update).astype(jnp.bfloat16)

    batch_size = 1
    batch_count = member_count // batch_size
    tick_count = section_count + batch_count - 1

    def tick(tick_index, carry):
        current_state, stored = carry
        received = shifted_2(current_state, "section", 1)
        first_rows = lax.dynamic_slice_in_dim(
            members, jnp.minimum(tick_index, batch_count - 1) * batch_size, batch_size, 0
        )
        incoming = jnp.where(section_index == 0, first_rows, received)
        result = sfno_block(incoming)
        position = tick_index - section_index
        is_valid = jnp.logical_and(position >= 0, position < batch_count)
        offset = jnp.clip(position, 0, batch_count - 1) * batch_size
        previous = lax.dynamic_slice_in_dim(stored, offset, batch_size, 0)
        stored = lax.dynamic_update_slice_in_dim(
            stored, jnp.where(is_valid, result, previous), offset, 0
        )
        return (result, stored)

    empty_state = jnp.zeros((batch_size,) + members.shape[1:], jnp.bfloat16)
    _, stored = lax.fori_loop(0, tick_count, tick, (empty_state, jnp.zeros_like(members)))
    merged = stored.reshape(stored.shape[0], stored.shape[1], stored.shape[2] * stored.shape[3])
    return merged[None]


def solution(mesh):
    return jax.shard_map(
        per_device,
        mesh=mesh,
        in_specs=(
            P("sht", None, "section"),
            P(None, "sht", None, "section"),
            P("section", None),
            P("section", None, None),
            P("section", None, None),
            P("section", None),
            P("section", None, None),
            P("section", None, None),
        ),
        out_specs=P("section", None, "sht", None),
        check_vma=False,
    )
```

profile of v0, /device:TPU:1, one launch (start us, length us, event | category | flops | bytes accessed | tf_op | source)
XLA Modules:
  0.0 957.9 jit_solution(10387569097498065270)
XLA Ops:
  2.8 10.9 %all-to-all-start.2 = ((bf16[8,7,2,256,24]{3,4,2,1,0:T(8,128)(2,1)}), bf16[8,7,2,256,24]{3,4,2,1,0:T(8,128)(2,1)S(1)}, u32[]{:S(2)}, u32[]{:S(2)}) async-start(bf16[8,7,2,256,24]{3,4,2,1,0:T(8,128)(2,1)} %broadcast_in_dim.440), calls=%async_computation.2 | async-start | bytes 2752512 | tf_op jit(solution)/shard_map/all_to_all | solution.py:17
  13.7 268.8 %while.39 = (s32[]{:T(128)}, f32[128,2]{0,1:T(2,128)S(1)}, f32[128,2]{0,1:T(2,128)S(1)}, f32[16,8,128,2]{2,3,1,0:T(2,128)S(1)}, s32[16,8]{0,1:T(8,128)S(1)}, /*i...) while((s32[]{:T(128)}, f32[128,2]{0,1:T(2,128)S(1)}, ...), condition=%wide.region_4.5_spmd.clone.clone.clone.clone, body=%wide.region_3.4_spmd.clone.clone.clone.clone.sunk | while | flops 20554 | bytes 85778 | solution.py:84
  286.6 667.2 %while.38 = (s32[]{:T(128)}, bf16[1,2,256,192]{2,3,1,0:T(8,128)(2,1)S(1)}, bf16[6,2,256,192]{2,3,1,0:T(8,128)(2,1)S(1)}, pred[]{:T(512)}, bf16[6,2,256,192]{2,3,...) while((s32[]{:T(128)}, ...), condition=%wide.region_10.11_spmd.clone, body=%wide.region_5.10_spmd.clone.sunk | while | flops 362546176 | bytes 24005356 | solution.py:219
  295.1 12.2 %all-to-all-start = ((bf16[1,2,128,384]{3,1,0,2:T(2,128)(2,1)}), bf16[1,2,128,384]{3,1,0,2:T(2,128)(2,1)S(1)}, u32[]{:S(2)}, u32[]{:S(2)}) async-start(bf16[1,2,128,384]{3,1,0,2:T(2,128)(2,1)} %copy.86), calls=%async_computation | async-start | bytes 393216 | tf_op jit(solution)/shard_map/while/body/eval_jaxpr/all_to_all | solution.py:162
  307.4 10.9 %all-to-all-done = bf16[1,2,128,384]{3,1,0,2:T(2,128)(2,1)S(1)} async-done(((bf16[1,2,128,384]{3,1,0,2:T(2,128)(2,1)}), bf16[1,2,128,384]{3,1,0,2:T(2,128)(2,1)S(1)}, u32[]{:S(2)}, u32[]{:S(2)}) %all-to-all-start) | async-done | bytes 196640 | tf_op jit(solution)/shard_map/while/body/eval_jaxpr/all_to_all | solution.py:162
  319.9 5.7 all-to-all-start.1
  325.8 10.7 %all-to-all-done.1 = bf16[1,128,2,384]{3,2,0,1:T(2,128)(2,1)S(1)} async-done(((bf16[1,128,2,384]{3,2,0,1:T(2,128)(2,1)}), bf16[1,128,2,384]{3,2,0,1:T(2,128)(2,1)S(1)}, u32[]{:S(2)}, u32[]{:S(2)}) %all-to-all-start.1) | async-done | bytes 196640 | tf_op jit(solution)/shard_map/while/body/eval_jaxpr/all_to_all | solution.py:176
  351.4 6.3 all-to-all-start
  357.7 10.9 %all-to-all-done = bf16[1,2,128,384]{3,1,0,2:T(2,128)(2,1)S(1)} async-done(((bf16[1,2,128,384]{3,1,0,2:T(2,128)(2,1)}), bf16[1,2,128,384]{3,1,0,2:T(2,128)(2,1)S(1)}, u32[]{:S(2)}, u32[]{:S(2)}) %all-to-all-start) | async-done | bytes 196640 | tf_op jit(solution)/shard_map/while/body/eval_jaxpr/all_to_all | solution.py:162
  370.2 5.7 all-to-all-start.1
  376.1 10.7 %all-to-all-done.1 = bf16[1,128,2,384]{3,2,0,1:T(2,128)(2,1)S(1)} async-done(((bf16[1,128,2,384]{3,2,0,1:T(2,128)(2,1)}), bf16[1,128,2,384]{3,2,0,1:T(2,128)(2,1)S(1)}, u32[]{:S(2)}, u32[]{:S(2)}) %all-to-all-start.1) | async-done | bytes 196640 | tf_op jit(solution)/shard_map/while/body/eval_jaxpr/all_to_all | solution.py:176
  401.7 6.3 all-to-all-start
  408.0 10.9 %all-to-all-done = bf16[1,2,128,384]{3,1,0,2:T(2,128)(2,1)S(1)} async-done(((bf16[1,2,128,384]{3,1,0,2:T(2,128)(2,1)}), bf16[1,2,128,384]{3,1,0,2:T(2,128)(2,1)S(1)}, u32[]{:S(2)}, u32[]{:S(2)}) %all-to-all-start) | async-done | bytes 196640 | tf_op jit(solution)/shard_map/while/body/eval_jaxpr/all_to_all | solution.py:162
  420.5 5.7 all-to-all-start.1
  426.4 10.7 %all-to-all-done.1 = bf16[1,128,2,384]{3,2,0,1:T(2,128)(2,1)S(1)} async-done(((bf16[1,128,2,384]{3,2,0,1:T(2,128)(2,1)}), bf16[1,128,2,384]{3,2,0,1:T(2,128)(2,1)S(1)}, u32[]{:S(2)}, u32[]{:S(2)}) %all-to-all-start.1) | async-done | bytes 196640 | tf_op jit(solution)/shard_map/while/body/eval_jaxpr/all_to_all | solution.py:176
  452.0 6.3 all-to-all-start
  458.3 10.9 %all-to-all-done = bf16[1,2,128,384]{3,1,0,2:T(2,128)(2,1)S(1)} async-done(((bf16[1,2,128,384]{3,1,0,2:T(2,128)(2,1)}), bf16[1,2,128,384]{3,1,0,2:T(2,128)(2,1)S(1)}, u32[]{:S(2)}, u32[]{:S(2)}) %all-to-all-start) | async-done | bytes 196640 | tf_op jit(solution)/shard_map/while/body/eval_jaxpr/all_to_all | solution.py:162
  470.8 5.7 all-to-all-start.1
  476.7 10.7 %all-to-all-done.1 = bf16[1,128,2,384]{3,2,0,1:T(2,128)(2,1)S(1)} async-done(((bf16[1,128,2,384]{3,2,0,1:T(2,128)(2,1)}), bf16[1,128,2,384]{3,2,0,1:T(2,128)(2,1)S(1)}, u32[]{:S(2)}, u32[]{:S(2)}) %all-to-all-start.1) | async-done | bytes 196640 | tf_op jit(solution)/shard_map/while/body/eval_jaxpr/all_to_all | solution.py:176
  502.3 6.3 all-to-all-start
  508.6 10.9 %all-to-all-done = bf16[1,2,128,384]{3,1,0,2:T(2,128)(2,1)S(1)} async-done(((bf16[1,2,128,384]{3,1,0,2:T(2,128)(2,1)}), bf16[1,2,128,384]{3,1,0,2:T(2,128)(2,1)S(1)}, u32[]{:S(2)}, u32[]{:S(2)}) %all-to-all-start) | async-done | bytes 196640 | tf_op jit(solution)/shard_map/while/body/eval_jaxpr/all_to_all | solution.py:162
  521.1 5.7 all-to-all-start.1
  527.1 10.7 %all-to-all-done.1 = bf16[1,128,2,384]{3,2,0,1:T(2,128)(2,1)S(1)} async-done(((bf16[1,128,2,384]{3,2,0,1:T(2,128)(2,1)}), bf16[1,128,2,384]{3,2,0,1:T(2,128)(2,1)S(1)}, u32[]{:S(2)}, u32[]{:S(2)}) %all-to-all-start.1) | async-done | bytes 196640 | tf_op jit(solution)/shard_map/while/body/eval_jaxpr/all_to_all | solution.py:176
  553.2 6.3 all-to-all-start
  559.5 10.9 %all-to-all-done = bf16[1,2,128,384]{3,1,0,2:T(2,128)(2,1)S(1)} async-done(((bf16[1,2,128,384]{3,1,0,2:T(2,128)(2,1)}), bf16[1,2,128,384]{3,1,0,2:T(2,128)(2,1)S(1)}, u32[]{:S(2)}, u32[]{:S(2)}) %all-to-all-start) | async-done | bytes 196640 | tf_op jit(solution)/shard_map/while/body/eval_jaxpr/all_to_all | solution.py:162
  572.0 5.7 all-to-all-start.1
  577.9 10.7 %all-to-all-done.1 = bf16[1,128,2,384]{3,2,0,1:T(2,128)(2,1)S(1)} async-done(((bf16[1,128,2,384]{3,2,0,1:T(2,128)(2,1)}), bf16[1,128,2,384]{3,2,0,1:T(2,128)(2,1)S(1)}, u32[]{:S(2)}, u32[]{:S(2)}) %all-to-all-start.1) | async-done | bytes 196640 | tf_op jit(solution)/shard_map/while/body/eval_jaxpr/all_to_all | solution.py:176
  604.7 6.3 all-to-all-start
  611.0 10.9 %all-to-all-done = bf16[1,2,128,384]{3,1,0,2:T(2,128)(2,1)S(1)} async-done(((bf16[1,2,128,384]{3,1,0,2:T(2,128)(2,1)}), bf16[1,2,128,384]{3,1,0,2:T(2,128)(2,1)S(1)}, u32[]{:S(2)}, u32[]{:S(2)}) %all-to-all-start) | async-done | bytes 196640 | tf_op jit(solution)/shard_map/while/body/eval_jaxpr/all_to_all | solution.py:162
  629.4 10.7 %all-to-all-done.1 = bf16[1,128,2,384]{3,2,0,1:T(2,128)(2,1)S(1)} async-done(((bf16[1,128,2,384]{3,2,0,1:T(2,128)(2,1)}), bf16[1,128,2,384]{3,2,0,1:T(2,128)(2,1)S(1)}, u32[]{:S(2)}, u32[]{:S(2)}) %all-to-all-start.1) | async-done | bytes 196640 | tf_op jit(solution)/shard_map/while/body/eval_jaxpr/all_to_all | solution.py:176
  656.2 6.3 all-to-all-start
  662.5 10.9 %all-to-all-done = bf16[1,2,128,384]{3,1,0,2:T(2,128)(2,1)S(1)} async-done(((bf16[1,2,128,384]{3,1,0,2:T(2,128)(2,1)}), bf16[1,2,128,384]{3,1,0,2:T(2,128)(2,1)S(1)}, u32[]{:S(2)}, u32[]{:S(2)}) %all-to-all-start) | async-done | bytes 196640 | tf_op jit(solution)/shard_map/while/body/eval_jaxpr/all_to_all | solution.py:162
  681.0 10.7 %all-to-all-done.1 = bf16[1,128,2,384]{3,2,0,1:T(2,128)(2,1)S(1)} async-done(((bf16[1,128,2,384]{3,2,0,1:T(2,128)(2,1)}), bf16[1,128,2,384]{3,2,0,1:T(2,128)(2,1)S(1)}, u32[]{:S(2)}, u32[]{:S(2)}) %all-to-all-start.1) | async-done | bytes 196640 | tf_op jit(solution)/shard_map/while/body/eval_jaxpr/all_to_all | solution.py:176
  707.7 6.3 all-to-all-start
  714.0 10.9 %all-to-all-done = bf16[1,2,128,384]{3,1,0,2:T(2,128)(2,1)S(1)} async-done(((bf16[1,2,128,384]{3,1,0,2:T(2,128)(2,1)}), bf16[1,2,128,384]{3,1,0,2:T(2,128)(2,1)S(1)}, u32[]{:S(2)}, u32[]{:S(2)}) %all-to-all-start) | async-done | bytes 196640 | tf_op jit(solution)/shard_map/while/body/eval_jaxpr/all_to_all | solution.py:162
  732.5 10.7 %all-to-all-done.1 = bf16[1,128,2,384]{3,2,0,1:T(2,128)(2,1)S(1)} async-done(((bf16[1,128,2,384]{3,2,0,1:T(2,128)(2,1)}), bf16[1,128,2,384]{3,2,0,1:T(2,128)(2,1)S(1)}, u32[]{:S(2)}, u32[]{:S(2)}) %all-to-all-start.1) | async-done | bytes 196640 | tf_op jit(solution)/shard_map/while/body/eval_jaxpr/all_to_all | solution.py:176
  759.2 6.3 all-to-all-start
  765.5 10.9 %all-to-all-done = bf16[1,2,128,384]{3,1,0,2:T(2,128)(2,1)S(1)} async-done(((bf16[1,2,128,384]{3,1,0,2:T(2,128)(2,1)}), bf16[1,2,128,384]{3,1,0,2:T(2,128)(2,1)S(1)}, u32[]{:S(2)}, u32[]{:S(2)}) %all-to-all-start) | async-done | bytes 196640 | tf_op jit(solution)/shard_map/while/body/eval_jaxpr/all_to_all | solution.py:162
  784.0 10.7 %all-to-all-done.1 = bf16[1,128,2,384]{3,2,0,1:T(2,128)(2,1)S(1)} async-done(((bf16[1,128,2,384]{3,2,0,1:T(2,128)(2,1)}), bf16[1,128,2,384]{3,2,0,1:T(2,128)(2,1)S(1)}, u32[]{:S(2)}, u32[]{:S(2)}) %all-to-all-start.1) | async-done | bytes 196640 | tf_op jit(solution)/shard_map/while/body/eval_jaxpr/all_to_all | solution.py:176
  810.8 6.3 all-to-all-start
  817.1 10.9 %all-to-all-done = bf16[1,2,128,384]{3,1,0,2:T(2,128)(2,1)S(1)} async-done(((bf16[1,2,128,384]{3,1,0,2:T(2,128)(2,1)}), bf16[1,2,128,384]{3,1,0,2:T(2,128)(2,1)S(1)}, u32[]{:S(2)}, u32[]{:S(2)}) %all-to-all-start) | async-done | bytes 196640 | tf_op jit(solution)/shard_map/while/body/eval_jaxpr/all_to_all | solution.py:162
  835.5 10.7 %all-to-all-done.1 = bf16[1,128,2,384]{3,2,0,1:T(2,128)(2,1)S(1)} async-done(((bf16[1,128,2,384]{3,2,0,1:T(2,128)(2,1)}), bf16[1,128,2,384]{3,2,0,1:T(2,128)(2,1)S(1)}, u32[]{:S(2)}, u32[]{:S(2)}) %all-to-all-start.1) | async-done | bytes 196640 | tf_op jit(solution)/shard_map/while/body/eval_jaxpr/all_to_all | solution.py:176
  862.3 6.3 all-to-all-start
  868.6 10.9 %all-to-all-done = bf16[1,2,128,384]{3,1,0,2:T(2,128)(2,1)S(1)} async-done(((bf16[1,2,128,384]{3,1,0,2:T(2,128)(2,1)}), bf16[1,2,128,384]{3,1,0,2:T(2,128)(2,1)S(1)}, u32[]{:S(2)}, u32[]{:S(2)}) %all-to-all-start) | async-done | bytes 196640 | tf_op jit(solution)/shard_map/while/body/eval_jaxpr/all_to_all | solution.py:162
  887.0 10.7 %all-to-all-done.1 = bf16[1,128,2,384]{3,2,0,1:T(2,128)(2,1)S(1)} async-done(((bf16[1,128,2,384]{3,2,0,1:T(2,128)(2,1)}), bf16[1,128,2,384]{3,2,0,1:T(2,128)(2,1)S(1)}, u32[]{:S(2)}, u32[]{:S(2)}) %all-to-all-start.1) | async-done | bytes 196640 | tf_op jit(solution)/shard_map/while/body/eval_jaxpr/all_to_all | solution.py:176
  913.8 6.3 all-to-all-start
  920.1 10.9 %all-to-all-done = bf16[1,2,128,384]{3,1,0,2:T(2,128)(2,1)S(1)} async-done(((bf16[1,2,128,384]{3,1,0,2:T(2,128)(2,1)}), bf16[1,2,128,384]{3,1,0,2:T(2,128)(2,1)S(1)}, u32[]{:S(2)}, u32[]{:S(2)}) %all-to-all-start) | async-done | bytes 196640 | tf_op jit(solution)/shard_map/while/body/eval_jaxpr/all_to_all | solution.py:162
  938.6 10.7 %all-to-all-done.1 = bf16[1,128,2,384]{3,2,0,1:T(2,128)(2,1)S(1)} async-done(((bf16[1,128,2,384]{3,2,0,1:T(2,128)(2,1)}), bf16[1,128,2,384]{3,2,0,1:T(2,128)(2,1)S(1)}, u32[]{:S(2)}, u32[]{:S(2)}) %all-to-all-start.1) | async-done | bytes 196640 | tf_op jit(solution)/shard_map/while/body/eval_jaxpr/all_to_all | solution.py:176
  (1023 shorter events, 458.1 us)
Async XLA Ops:
  2.8 282.2 %all-to-all-start.2 = ((bf16[8,7,2,256,24]{3,4,2,1,0:T(8,128)(2,1)}), bf16[8,7,2,256,24]{3,4,2,1,0:T(8,128)(2,1)S(1)}, u32[]{:S(2)}, u32[]{:S(2)}) async-start(bf16[8,7,2,256,24]{3,4,2,1,0:T(8,128)(2,1)} %broadcast_in_dim.440), calls=%async_computation.2 | async-start | bytes 2752512 | tf_op jit(solution)/shard_map/all_to_all | solution.py:17
  13.7 268.9 %copy-start.3 = (f32[1,2,24576]{2,1,0:T(2,128)S(1)}, f32[1,2,24576]{2,1,0:T(2,128)}, u32[]{:S(2)}) copy-start(f32[1,2,24576]{2,1,0:T(2,128)} %param.15) | copy-start | bytes 589828
  13.7 269.2 %copy-start.4 = (bf16[1,192,192]{2,1,0:T(8,128)(2,1)S(1)}, bf16[1,192,192]{2,1,0:T(8,128)(2,1)}, u32[]{:S(2)}) copy-start(bf16[1,192,192]{2,1,0:T(8,128)(2,1)} %param.16) | copy-start | bytes 221188
  286.6 6.3 collective-permute-start
  295.1 23.2 %all-to-all-start = ((bf16[1,2,128,384]{3,1,0,2:T(2,128)(2,1)}), bf16[1,2,128,384]{3,1,0,2:T(2,128)(2,1)S(1)}, u32[]{:S(2)}, u32[]{:S(2)}) async-start(bf16[1,2,128,384]{3,1,0,2:T(2,128)(2,1)} %copy.86), calls=%async_computation | async-start | bytes 393216 | tf_op jit(solution)/shard_map/while/body/eval_jaxpr/all_to_all | solution.py:162
  319.9 16.6 %all-to-all-start.1 = ((bf16[1,128,2,384]{3,2,0,1:T(2,128)(2,1)}), bf16[1,128,2,384]{3,2,0,1:T(2,128)(2,1)S(1)}, u32[]{:S(2)}, u32[]{:S(2)}) async-start(bf16[1,128,2,384]{3,2,0,1:T(2,128)(2,1)} %copy.88), calls=%async_computation.1 | async-start | bytes 393216 | tf_op jit(solution)/shard_map/while/body/eval_jaxpr/all_to_all | solution.py:176
  341.1 8.1 collective-permute-start
  351.4 17.2 %all-to-all-start = ((bf16[1,2,128,384]{3,1,0,2:T(2,128)(2,1)}), bf16[1,2,128,384]{3,1,0,2:T(2,128)(2,1)S(1)}, u32[]{:S(2)}, u32[]{:S(2)}) async-start(bf16[1,2,128,384]{3,1,0,2:T(2,128)(2,1)} %copy.86), calls=%async_computation | async-start | bytes 393216 | tf_op jit(solution)/shard_map/while/body/eval_jaxpr/all_to_all | solution.py:162
  370.2 16.6 %all-to-all-start.1 = ((bf16[1,128,2,384]{3,2,0,1:T(2,128)(2,1)}), bf16[1,128,2,384]{3,2,0,1:T(2,128)(2,1)S(1)}, u32[]{:S(2)}, u32[]{:S(2)}) async-start(bf16[1,128,2,384]{3,2,0,1:T(2,128)(2,1)} %copy.88), calls=%async_computation.1 | async-start | bytes 393216 | tf_op jit(solution)/shard_map/while/body/eval_jaxpr/all_to_all | solution.py:176
  391.4 8.1 collective-permute-start
  401.7 17.2 %all-to-all-start = ((bf16[1,2,128,384]{3,1,0,2:T(2,128)(2,1)}), bf16[1,2,128,384]{3,1,0,2:T(2,128)(2,1)S(1)}, u32[]{:S(2)}, u32[]{:S(2)}) async-start(bf16[1,2,128,384]{3,1,0,2:T(2,128)(2,1)} %copy.86), calls=%async_computation | async-start | bytes 393216 | tf_op jit(solution)/shard_map/while/body/eval_jaxpr/all_to_all | solution.py:162
  420.5 16.6 %all-to-all-start.1 = ((bf16[1,128,2,384]{3,2,0,1:T(2,128)(2,1)}), bf16[1,128,2,384]{3,2,0,1:T(2,128)(2,1)S(1)}, u32[]{:S(2)}, u32[]{:S(2)}) async-start(bf16[1,128,2,384]{3,2,0,1:T(2,128)(2,1)} %copy.88), calls=%async_computation.1 | async-start | bytes 393216 | tf_op jit(solution)/shard_map/while/body/eval_jaxpr/all_to_all | solution.py:176
  441.7 8.1 collective-permute-start
  452.0 17.2 %all-to-all-start = ((bf16[1,2,128,384]{3,1,0,2:T(2,128)(2,1)}), bf16[1,2,128,384]{3,1,0,2:T(2,128)(2,1)S(1)}, u32[]{:S(2)}, u32[]{:S(2)}) async-start(bf16[1,2,128,384]{3,1,0,2:T(2,128)(2,1)} %copy.86), calls=%async_computation | async-start | bytes 393216 | tf_op jit(solution)/shard_map/while/body/eval_jaxpr/all_to_all | solution.py:162
  470.8 16.6 %all-to-all-start.1 = ((bf16[1,128,2,384]{3,2,0,1:T(2,128)(2,1)}), bf16[1,128,2,384]{3,2,0,1:T(2,128)(2,1)S(1)}, u32[]{:S(2)}, u32[]{:S(2)}) async-start(bf16[1,128,2,384]{3,2,0,1:T(2,128)(2,1)} %copy.88), calls=%async_computation.1 | async-start | bytes 393216 | tf_op jit(solution)/shard_map/while/body/eval_jaxpr/all_to_all | solution.py:176
  492.0 8.1 collective-permute-start
  502.3 17.2 %all-to-all-start = ((bf16[1,2,128,384]{3,1,0,2:T(2,128)(2,1)}), bf16[1,2,128,384]{3,1,0,2:T(2,128)(2,1)S(1)}, u32[]{:S(2)}, u32[]{:S(2)}) async-start(bf16[1,2,128,384]{3,1,0,2:T(2,128)(2,1)} %copy.86), calls=%async_computation | async-start | bytes 393216 | tf_op jit(solution)/shard_map/while/body/eval_jaxpr/all_to_all | solution.py:162
  521.1 16.6 %all-to-all-start.1 = ((bf16[1,128,2,384]{3,2,0,1:T(2,128)(2,1)}), bf16[1,128,2,384]{3,2,0,1:T(2,128)(2,1)S(1)}, u32[]{:S(2)}, u32[]{:S(2)}) async-start(bf16[1,128,2,384]{3,2,0,1:T(2,128)(2,1)} %copy.88), calls=%async_computation.1 | async-start | bytes 393216 | tf_op jit(solution)/shard_map/while/body/eval_jaxpr/all_to_all | solution.py:176
  542.3 8.6 collective-permute-start
  553.2 17.2 %all-to-all-start = ((bf16[1,2,128,384]{3,1,0,2:T(2,128)(2,1)}), bf16[1,2,128,384]{3,1,0,2:T(2,128)(2,1)S(1)}, u32[]{:S(2)}, u32[]{:S(2)}) async-start(bf16[1,2,128,384]{3,1,0,2:T(2,128)(2,1)} %copy.86), calls=%async_computation | async-start | bytes 393216 | tf_op jit(solution)/shard_map/while/body/eval_jaxpr/all_to_all | solution.py:162
  572.0 16.6 %all-to-all-start.1 = ((bf16[1,128,2,384]{3,2,0,1:T(2,128)(2,1)}), bf16[1,128,2,384]{3,2,0,1:T(2,128)(2,1)S(1)}, u32[]{:S(2)}, u32[]{:S(2)}) async-start(bf16[1,128,2,384]{3,2,0,1:T(2,128)(2,1)} %copy.88), calls=%async_computation.1 | async-start | bytes 393216 | tf_op jit(solution)/shard_map/while/body/eval_jaxpr/all_to_all | solution.py:176
  593.2 11.5 %copy-start = (bf16[6,2,256,192]{2,3,1,0:T(8,128)(2,1)}, bf16[6,2,256,192]{2,3,1,0:T(8,128)(2,1)S(1)}, u32[]{:S(2)}) copy-start(bf16[6,2,256,192]{2,3,1,0:T(8,128)(2,1)S(1)} %get-tuple-element.1308) | copy-start | bytes 3538948 | tf_op jit(solution)/shard_map/while
  593.2 9.3 collective-permute-start
  604.7 17.2 %all-to-all-start = ((bf16[1,2,128,384]{3,1,0,2:T(2,128)(2,1)}), bf16[1,2,128,384]{3,1,0,2:T(2,128)(2,1)S(1)}, u32[]{:S(2)}, u32[]{:S(2)}) async-start(bf16[1,2,128,384]{3,1,0,2:T(2,128)(2,1)} %copy.86), calls=%async_computation | async-start | bytes 393216 | tf_op jit(solution)/shard_map/while/body/eval_jaxpr/all_to_all | solution.py:162
  623.5 16.6 %all-to-all-start.1 = ((bf16[1,128,2,384]{3,2,0,1:T(2,128)(2,1)}), bf16[1,128,2,384]{3,2,0,1:T(2,128)(2,1)S(1)}, u32[]{:S(2)}, u32[]{:S(2)}) async-start(bf16[1,128,2,384]{3,2,0,1:T(2,128)(2,1)} %copy.88), calls=%async_computation.1 | async-start | bytes 393216 | tf_op jit(solution)/shard_map/while/body/eval_jaxpr/all_to_all | solution.py:176
  644.7 11.5 %copy-start = (bf16[6,2,256,192]{2,3,1,0:T(8,128)(2,1)}, bf16[6,2,256,192]{2,3,1,0:T(8,128)(2,1)S(1)}, u32[]{:S(2)}) copy-start(bf16[6,2,256,192]{2,3,1,0:T(8,128)(2,1)S(1)} %get-tuple-element.1308) | copy-start | bytes 3538948 | tf_op jit(solution)/shard_map/while
  644.7 9.3 collective-permute-start
  656.2 17.2 %all-to-all-start = ((bf16[1,2,128,384]{3,1,0,2:T(2,128)(2,1)}), bf16[1,2,128,384]{3,1,0,2:T(2,128)(2,1)S(1)}, u32[]{:S(2)}, u32[]{:S(2)}) async-start(bf16[1,2,128,384]{3,1,0,2:T(2,128)(2,1)} %copy.86), calls=%async_computation | async-start | bytes 393216 | tf_op jit(solution)/shard_map/while/body/eval_jaxpr/all_to_all | solution.py:162
  675.0 16.6 %all-to-all-start.1 = ((bf16[1,128,2,384]{3,2,0,1:T(2,128)(2,1)}), bf16[1,128,2,384]{3,2,0,1:T(2,128)(2,1)S(1)}, u32[]{:S(2)}, u32[]{:S(2)}) async-start(bf16[1,128,2,384]{3,2,0,1:T(2,128)(2,1)} %copy.88), calls=%async_computation.1 | async-start | bytes 393216 | tf_op jit(solution)/shard_map/while/body/eval_jaxpr/all_to_all | solution.py:176
  696.2 11.5 %copy-start = (bf16[6,2,256,192]{2,3,1,0:T(8,128)(2,1)}, bf16[6,2,256,192]{2,3,1,0:T(8,128)(2,1)S(1)}, u32[]{:S(2)}) copy-start(bf16[6,2,256,192]{2,3,1,0:T(8,128)(2,1)S(1)} %get-tuple-element.1308) | copy-start | bytes 3538948 | tf_op jit(solution)/shard_map/while
  696.3 9.3 collective-permute-start
  707.7 17.2 %all-to-all-start = ((bf16[1,2,128,384]{3,1,0,2:T(2,128)(2,1)}), bf16[1,2,128,384]{3,1,0,2:T(2,128)(2,1)S(1)}, u32[]{:S(2)}, u32[]{:S(2)}) async-start(bf16[1,2,128,384]{3,1,0,2:T(2,128)(2,1)} %copy.86), calls=%async_computation | async-start | bytes 393216 | tf_op jit(solution)/shard_map/while/body/eval_jaxpr/all_to_all | solution.py:162
  726.5 16.6 %all-to-all-start.1 = ((bf16[1,128,2,384]{3,2,0,1:T(2,128)(2,1)}), bf16[1,128,2,384]{3,2,0,1:T(2,128)(2,1)S(1)}, u32[]{:S(2)}, u32[]{:S(2)}) async-start(bf16[1,128,2,384]{3,2,0,1:T(2,128)(2,1)} %copy.88), calls=%async_computation.1 | async-start | bytes 393216 | tf_op jit(solution)/shard_map/while/body/eval_jaxpr/all_to_all | solution.py:176
  747.7 11.5 %copy-start = (bf16[6,2,256,192]{2,3,1,0:T(8,128)(2,1)}, bf16[6,2,256,192]{2,3,1,0:T(8,128)(2,1)S(1)}, u32[]{:S(2)}) copy-start(bf16[6,2,256,192]{2,3,1,0:T(8,128)(2,1)S(1)} %get-tuple-element.1308) | copy-start | bytes 3538948 | tf_op jit(solution)/shard_map/while
  747.8 9.3 collective-permute-start
  759.2 17.2 %all-to-all-start = ((bf16[1,2,128,384]{3,1,0,2:T(2,128)(2,1)}), bf16[1,2,128,384]{3,1,0,2:T(2,128)(2,1)S(1)}, u32[]{:S(2)}, u32[]{:S(2)}) async-start(bf16[1,2,128,384]{3,1,0,2:T(2,128)(2,1)} %copy.86), calls=%async_computation | async-start | bytes 393216 | tf_op jit(solution)/shard_map/while/body/eval_jaxpr/all_to_all | solution.py:162
  778.1 16.6 %all-to-all-start.1 = ((bf16[1,128,2,384]{3,2,0,1:T(2,128)(2,1)}), bf16[1,128,2,384]{3,2,0,1:T(2,128)(2,1)S(1)}, u32[]{:S(2)}, u32[]{:S(2)}) async-start(bf16[1,128,2,384]{3,2,0,1:T(2,128)(2,1)} %copy.88), calls=%async_computation.1 | async-start | bytes 393216 | tf_op jit(solution)/shard_map/while/body/eval_jaxpr/all_to_all | solution.py:176
  799.3 11.5 %copy-start = (bf16[6,2,256,192]{2,3,1,0:T(8,128)(2,1)}, bf16[6,2,256,192]{2,3,1,0:T(8,128)(2,1)S(1)}, u32[]{:S(2)}) copy-start(bf16[6,2,256,192]{2,3,1,0:T(8,128)(2,1)S(1)} %get-tuple-element.1308) | copy-start | bytes 3538948 | tf_op jit(solution)/shard_map/while
  799.3 9.3 collective-permute-start
  810.8 17.2 %all-to-all-start = ((bf16[1,2,128,384]{3,1,0,2:T(2,128)(2,1)}), bf16[1,2,128,384]{3,1,0,2:T(2,128)(2,1)S(1)}, u32[]{:S(2)}, u32[]{:S(2)}) async-start(bf16[1,2,128,384]{3,1,0,2:T(2,128)(2,1)} %copy.86), calls=%async_computation | async-start | bytes 393216 | tf_op jit(solution)/shard_map/while/body/eval_jaxpr/all_to_all | solution.py:162
  829.6 16.6 %all-to-all-start.1 = ((bf16[1,128,2,384]{3,2,0,1:T(2,128)(2,1)}), bf16[1,128,2,384]{3,2,0,1:T(2,128)(2,1)S(1)}, u32[]{:S(2)}, u32[]{:S(2)}) async-start(bf16[1,128,2,384]{3,2,0,1:T(2,128)(2,1)} %copy.88), calls=%async_computation.1 | async-start | bytes 393216 | tf_op jit(solution)/shard_map/while/body/eval_jaxpr/all_to_all | solution.py:176
  850.8 11.5 %copy-start = (bf16[6,2,256,192]{2,3,1,0:T(8,128)(2,1)}, bf16[6,2,256,192]{2,3,1,0:T(8,128)(2,1)S(1)}, u32[]{:S(2)}) copy-start(bf16[6,2,256,192]{2,3,1,0:T(8,128)(2,1)S(1)} %get-tuple-element.1308) | copy-start | bytes 3538948 | tf_op jit(solution)/shard_map/while
  850.8 9.3 collective-permute-start
  862.3 17.2 %all-to-all-start = ((bf16[1,2,128,384]{3,1,0,2:T(2,128)(2,1)}), bf16[1,2,128,384]{3,1,0,2:T(2,128)(2,1)S(1)}, u32[]{:S(2)}, u32[]{:S(2)}) async-start(bf16[1,2,128,384]{3,1,0,2:T(2,128)(2,1)} %copy.86), calls=%async_computation | async-start | bytes 393216 | tf_op jit(solution)/shard_map/while/body/eval_jaxpr/all_to_all | solution.py:162
  881.1 16.6 %all-to-all-start.1 = ((bf16[1,128,2,384]{3,2,0,1:T(2,128)(2,1)}), bf16[1,128,2,384]{3,2,0,1:T(2,128)(2,1)S(1)}, u32[]{:S(2)}, u32[]{:S(2)}) async-start(bf16[1,128,2,384]{3,2,0,1:T(2,128)(2,1)} %copy.88), calls=%async_computation.1 | async-start | bytes 393216 | tf_op jit(solution)/shard_map/while/body/eval_jaxpr/all_to_all | solution.py:176
  902.3 9.3 collective-permute-start
  913.8 17.2 %all-to-all-start = ((bf16[1,2,128,384]{3,1,0,2:T(2,128)(2,1)}), bf16[1,2,128,384]{3,1,0,2:T(2,128)(2,1)S(1)}, u32[]{:S(2)}, u32[]{:S(2)}) async-start(bf16[1,2,128,384]{3,1,0,2:T(2,128)(2,1)} %copy.86), calls=%async_computation | async-start | bytes 393216 | tf_op jit(solution)/shard_map/while/body/eval_jaxpr/all_to_all | solution.py:162
  932.6 16.6 %all-to-all-start.1 = ((bf16[1,128,2,384]{3,2,0,1:T(2,128)(2,1)}), bf16[1,128,2,384]{3,2,0,1:T(2,128)(2,1)S(1)}, u32[]{:S(2)}, u32[]{:S(2)}) async-start(bf16[1,128,2,384]{3,2,0,1:T(2,128)(2,1)} %copy.88), calls=%async_computation.1 | async-start | bytes 393216 | tf_op jit(solution)/shard_map/while/body/eval_jaxpr/all_to_all | solution.py:176
  (36 other events, 115.3 us)
where the time goes:
time: 967 us; the launch traced here: 958 us
  waiting for transfers between devices  331 us (34%)
  starting transfers between devices  234 us (24%)
  other arithmetic  184 us (19%)
  loops' own time  86.5 us (9%)
  matrix products  66.6 us (7%)
  local copies, waits for them, and re-layouts  55.9 us (6%)
    all_to_all x13, waiting for transfers between devices, spectral(): lax.all_to_all(spectrum, 'sht', split_axis=2, concat_axis=1, tiled=True)  142 us
    all_to_all x13, waiting for transfers between devices, spectral(): lax.all_to_all(returned, 'sht', split_axis=1, concat_axis=2, tiled=True)  139 us
    all_to_all x13, starting transfers between devices, spectral(): lax.all_to_all(spectrum, 'sht', split_axis=2, concat_axis=1, tiled=True)  87.6 us
    another operation x1, loops' own time, legendre_table(): lax.scan(advance, (initial, initial), jnp.arange(lmax, dtype=jnp.int32),...  83.6 us
    gt x128, other arithmetic, advance(): degree > m_index[None, :] + 1  80.2 us
    eq x64, other arithmetic, advance(): degree == m_index[None, :]  79.9 us
    all_to_all x13, starting transfers between devices, spectral(): lax.all_to_all(returned, 'sht', split_axis=1, concat_axis=2, tiled=True)  73.6 us
    ppermute x13, starting transfers between devices, shifted_2(): lax.ppermute(value, axis, [(source, source + steps) for source in range(f...  61.9 us
  transfers between devices with their start and end apart: 40, of which 39 were waited for; matrix products, arithmetic and copies ran while one was open for 20% of the time, Pallas kernels for 0%

commit v1 on v0

v1 whole, which is shorter than its diff:
```python
import math

import jax
import jax.numpy as jnp
from jax import lax
from jax.experimental import pallas as pl
from jax.sharding import PartitionSpec as P

C = 192
NLAT = 128
NLON = 256
LMAX = 128
MMAX = 128


def recurrence_kernel(lower_ref, upper_ref, first_ref, cosine_ref, diagonal_ref, table_ref):
    cosine = cosine_ref[...]
    diagonal = diagonal_ref[...]

    def advance(degree, carry):
        latest, earlier = carry
        current = (
            lower_ref[degree] * (cosine * latest - upper_ref[degree] * earlier)
            + first_ref[degree] * diagonal
        )
        table_ref[degree] = current
        return (current, latest)

    initial = cosine * 0.0
    lax.fori_loop(0, LMAX, advance, (initial, initial), unroll=8)


def legendre_table(m_first, m_count):
    latitudes = jnp.arange(NLAT, dtype=jnp.float32)
    colatitude = math.pi * (latitudes + 0.5) / NLAT
    cosine = jnp.cos(colatitude)
    sine = jnp.sin(colatitude)
    orders = jnp.arange(1, MMAX, dtype=jnp.float32)
    factors = jnp.cumsum(0.5 * jnp.log((2.0 * orders + 1.0) / (2.0 * orders)))
    log_diag = jnp.concatenate([jnp.zeros((1,), jnp.float32), factors])
    m_index = m_first + jnp.arange(m_count, dtype=jnp.int32)
    picked = jnp.sum(
        jnp.where(
            m_index[:, None] == jnp.arange(MMAX, dtype=jnp.int32)[None, :], log_diag[None, :], 0.0
        ),
        axis=1,
    )
    m_float = m_index.astype(jnp.float32)
    diagonal = jnp.exp(picked[:, None] + m_float[:, None] * jnp.log(sine)[None, :]) * math.sqrt(
        0.25 / math.pi
    )
    degree = jnp.arange(LMAX, dtype=jnp.float32)[:, None]
    order = m_float[None, :]
    lower = jnp.sqrt(
        jnp.maximum(4.0 * degree * degree - 1.0, 0.0)
        / jnp.maximum(degree * degree - order * order, 1.0)
    )
    shifted = degree - 1.0
    upper = jnp.sqrt(
        jnp.maximum(shifted * shifted - order * order, 0.0)
        / jnp.maximum(4.0 * shifted * shifted - 1.0, 1.0)
    )
    first = jnp.where(degree == order, 1.0, 0.0)
    wide = lambda x: jnp.broadcast_to(x[:, :, None], (LMAX, m_count, NLAT))
    table = pl.pallas_call(
        recurrence_kernel,
        out_shape=jax.ShapeDtypeStruct((LMAX, m_count, NLAT), jnp.float32),
    )(
        wide(lower),
        wide(upper),
        wide(first),
        jnp.broadcast_to(cosine[None, :], (m_count, NLAT)),
        diagonal,
    )
    weights = sine * (2.0 * math.pi / NLON) * (math.pi / NLAT)
    return (table, weights)


def fourier_tables(nlon, mmax):
    samples = jnp.arange(nlon, dtype=jnp.int32)
    orders = jnp.arange(mmax, dtype=jnp.int32)
    phase = (samples[:, None] * orders[None, :] % nlon).astype(jnp.float32) * (2.0 * math.pi / nlon)
    cosines = jnp.cos(phase)
    sines = jnp.sin(phase)
    forward = jnp.stack([cosines, -sines], axis=1).astype(jnp.bfloat16)
    factor = jnp.where(orders == 0, 1.0, 2.0).astype(jnp.float32)
    inverse = jnp.stack([cosines.T * factor[:, None], -sines.T * factor[:, None]], axis=0).astype(
        jnp.bfloat16
    )
    return (forward, inverse)


def layer_norm(values, gain_vector):
    average = jnp.mean(values, axis=-1, keepdims=True)
    centred = values - average
    variance = jnp.mean(centred * centred, axis=-1, keepdims=True)
    return centred * lax.rsqrt(variance + 1e-05) * gain_vector


def apply_gain(coeffs, gain_table):
    real_part = coeffs[:, :, :, 0]
    imag_part = coeffs[:, :, :, 1]
    gain_real = gain_table[0][None, :, None, :]
    gain_imag = gain_table[1][None, :, None, :]
    return jnp.stack(
        [
            real_part * gain_real - imag_part * gain_imag,
            real_part * gain_imag + imag_part * gain_real,
        ],
        axis=3,
    )


def recenter(analysis, perturbations):
    pert_wide = perturbations.astype(jnp.float32)
    average = jnp.mean(pert_wide, axis=0, keepdims=True)
    return (analysis.astype(jnp.float32)[None] + pert_wide - average).astype(jnp.bfloat16)


def per_device(
    analysis, perturbations, gain_first, spectral_gain, skip_weight, gain_second, mlp_in, mlp_out
):
    count = lax.axis_size("section")
    member_count = perturbations.shape[0]
    m_count = MMAX // lax.axis_size("sht")
    members = recenter(analysis, perturbations)
    members = jnp.pad(members, ((0, count - member_count), (0, 0), (0, 0), (0, 0)))
    slices = lax.all_to_all(members, "section", split_axis=0, concat_axis=0, tiled=True)
    state = jnp.moveaxis(slices, 0, 2).reshape(1, slices.shape[1], NLON, C)
    gains = lax.all_gather(jnp.concatenate([gain_first, gain_second], axis=0), "section")
    filters = lax.all_gather(spectral_gain[0].astype(jnp.bfloat16), "section")
    matrices = lax.all_gather(
        jnp.concatenate([skip_weight[0], mlp_in[0], mlp_out[0]], axis=1), "section"
    )
    pick = lambda stack, block: lax.dynamic_index_in_dim(stack, block, 0, keepdims=False)
    forward, inverse = fourier_tables(NLON, MMAX)
    legendre, weights = legendre_table(lax.axis_index("sht") * m_count, m_count)
    weighted = (legendre * weights[None, None, :]).astype(jnp.bfloat16)
    plain_table = legendre.astype(jnp.bfloat16)

    def spectral(normed, full_gain):
        batch_rows = normed.shape[0]
        lat_rows = normed.shape[1]
        spectrum = jnp.einsum(
            "bjkc,kpm->bjmpc", normed, forward, preferred_element_type=jnp.float32
        ).astype(jnp.bfloat16)
        spectrum = spectrum.reshape(batch_rows, lat_rows, MMAX, 2 * C)
        exchanged = lax.all_to_all(spectrum, "sht", split_axis=2, concat_axis=1, tiled=True)
        item_count = exchanged.shape[0]
        coeffs = jnp.einsum(
            "lmj,bjmq->blmq", weighted, exchanged, preferred_element_type=jnp.float32
        )
        coeffs = coeffs.reshape(item_count, LMAX, m_count, 2, C)
        filtered = (
            apply_gain(coeffs, full_gain)
            .astype(jnp.bfloat16)
            .reshape(item_count, LMAX, m_count, 2 * C)
        )
        returned = jnp.einsum(
            "lmj,blmq->bjmq", plain_table, filtered, preferred_element_type=jnp.float32
        ).astype(jnp.bfloat16)
        returned = lax.all_to_all(returned, "sht", split_axis=1, concat_axis=2, tiled=True)
        returned = returned.reshape(batch_rows, lat_rows, MMAX, 2, C)
        return jnp.einsum("bjmpc,pmk->bjkc", returned, inverse, preferred_element_type=jnp.float32)

    def step(block, carry):
        state, stored = carry
        block_matrices = pick(matrices, block)
        block_gains = pick(gains, block)
        full_gain = pick(filters, block).reshape(2, LMAX, C).astype(jnp.float32)
        skip = block_matrices[:, :C]
        first_matrix = block_matrices[:, C : 3 * C]
        second_matrix = block_matrices[:, 3 * C :]
        state_wide = state.astype(jnp.float32)
        normed = layer_norm(state_wide, block_gains[0]).astype(jnp.bfloat16)
        spatial = spectral(normed, full_gain)
        skipped = jnp.dot(
            normed.reshape(-1, C), skip, preferred_element_type=jnp.float32
        ).reshape(spatial.shape)
        activated = jax.nn.gelu(spatial + skipped, approximate=False)
        second = layer_norm(activated, block_gains[1]).astype(jnp.bfloat16)
        hidden = jax.nn.gelu(
            jnp.dot(second.reshape(-1, C), first_matrix, preferred_element_type=jnp.float32),
            approximate=False,
        ).astype(jnp.bfloat16)
        update = lax.dot_general(
            hidden, second_matrix, (((1,), (1,)), ((), ())), preferred_element_type=jnp.float32
        ).reshape(spatial.shape)
        state = (state_wide + update).astype(jnp.bfloat16)
        return (state, lax.dynamic_update_slice_in_dim(stored, state, block, 0))

    empty = jnp.zeros((count, *state.shape[1:]), jnp.bfloat16)
    _, stacked = lax.fori_loop(0, count, step, (state, empty))
    stored = lax.all_to_all(stacked, "section", split_axis=0, concat_axis=0, tiled=True)
    stored = stored[:member_count]
    return stored.reshape(1, member_count, stored.shape[1], NLON * C)


def solution(mesh):
    return jax.shard_map(
        per_device,
        mesh=mesh,
        in_specs=(
            P("sht", None, "section"),
            P(None, "sht", None, "section"),
            P("section", None),
            P("section", None, None),
            P("section", None, None),
            P("section", None),
            P("section", None, None),
            P("section", None, None),
        ),
        out_specs=P("section", None, "sht", None),
        check_vma=False,
    )
```

time: 967 us -> 475 us (0.49)
  waiting for transfers between devices: 331 us -> 155 us
  other arithmetic: 184 us -> 15.7 us
  starting transfers between devices: 234 us -> 108 us
  blocking collectives: 0 us -> 97.1 us
  loops' own time: 86.5 us -> 1.43 us
  matrix products: 66.6 us -> 33.4 us
  between operations: 0.26 us -> 13.6 us
    another operation x2 -> x1, loops' own time: 86.5 us -> 1.43 us  [per_device(): _, stacked = lax.fori_loop(0, count, step, (state, empty))]
    gt x128 -> x0, other arithmetic: 80.2 us -> none  [advance(): degree > m_index[None, :] + 1]
    eq x64 -> x0, other arithmetic: 79.9 us -> none  [advance(): degree == m_index[None, :]]
    all_to_all x13 -> x8, waiting for transfers between devices: 139 us -> 75.5 us  [spectral(): lax.all_to_all(returned, 'sht', split_axis=1, concat_axis=2, tiled=True)]
    all_to_all x13 -> x8, waiting for transfers between devices: 142 us -> 79.8 us  [spectral(): lax.all_to_all(spectrum, 'sht', split_axis=2, concat_axis=1, tiled=True)]
    ppermute x13 -> x0, starting transfers between devices: 61.9 us -> none  [shifted_2(): lax.ppermute(value, axis, [(source, source + steps) for source in range(f...]
    all_gather x0 -> x2, blocking collectives: none -> 52.5 us  [the longest x1 28 us: per_device(): filters = lax.all_gather(spectral_gain[0].astype(jnp.bfloat16), 'section')]
    ppermute x13 -> x0, waiting for transfers between devices: 50.1 us -> none  [shifted_2(): lax.ppermute(value, axis, [(source, source + steps) for source in range(f...]
  transfers between devices with their start and end apart: 40 -> 18, of which waited for: 39 -> 16; matrix products, arithmetic and copies ran while one was open for 20% -> 6% of each run, Pallas kernels for 0% -> 0%
where the time goes in v1:
time: 475 us; the launch traced here: 474 us
  waiting for transfers between devices  155 us (33%)
  starting transfers between devices  108 us (23%)
  blocking collectives  97.1 us (20%)
  local copies, waits for them, and re-layouts  46.8 us (10%)
  matrix products  33.4 us (7%)
  other arithmetic  15.7 us (3%)
  between operations  13.6 us (3%)
    all_to_all x8, waiting for transfers between devices, spectral(): lax.all_to_all(spectrum, 'sht', split_axis=2, concat_axis=1, tiled=True)  79.8 us
    all_to_all x8, waiting for transfers between devices, spectral(): lax.all_to_all(returned, 'sht', split_axis=1, concat_axis=2, tiled=True)  75.5 us
    all_to_all x8, starting transfers between devices, spectral(): lax.all_to_all(spectrum, 'sht', split_axis=2, concat_axis=1, tiled=True)  58 us
    all_to_all x8, starting transfers between devices, spectral(): lax.all_to_all(returned, 'sht', split_axis=1, concat_axis=2, tiled=True)  45.3 us
    all_to_all x1, blocking collectives, per_device(): lax.all_to_all(stacked, 'section', split_axis=0, concat_axis=0, tiled=True)  44.6 us
    all_gather x1, blocking collectives, per_device(): filters = lax.all_gather(spectral_gain[0].astype(jnp.bfloat16), 'section')  28 us
    all_gather x1, blocking collectives, per_device(): lax.all_gather(jnp.concatenate([gain_first, gain_second], axis=0), 'secti...  24.6 us
    dot_general x8, matrix products, step(): lax.dot_general(hidden, second_matrix, (((1,), (1,)), ((), ())), preferre...  17.3 us
  transfers between devices with their start and end apart: 18, of which 16 were waited for; matrix products, arithmetic and copies ran while one was open for 6% of the time, Pallas kernels for 0%

profile of v1, /device:TPU:1, one launch (start us, length us, event | category | flops | bytes accessed | tf_op | source)
XLA Modules:
  0.0 473.8 jit_solution(4867347555240384876)
XLA Ops:
  6.5 2.0 pad_maximum_fusion.1
  13.7 2.3 shard_map.82
  18.0 24.6 %all-gather.2 = f32[8,2,192]{2,1,0:T(2,128)S(1)} all-gather(f32[1,2,192]{2,1,0:T(2,128)S(1)} %maximum_bitcast_fusion), channel_id=2, replica_groups=mesh['section'=8,'sht'=64] {'section'}, dimensions={0}, use_global_device_ids=true | all-gather | bytes 13824 | tf_op jit(solution)/shard_map/all_gather | solution.py:130
  43.7 4.9 %all-to-all-start.2 = ((bf16[8,2,256,24]{2,3,1,0:T(8,128)(2,1)}), bf16[8,2,256,24]{2,3,1,0:T(8,128)(2,1)S(1)}, u32[]{:S(2)}, u32[]{:S(2)}) async-start(bf16[8,2,256,24]{2,3,1,0:T(8,128)(2,1)} %pad.4), calls=%async_computation.2 | async-start | bytes 393216 | tf_op jit(solution)/shard_map/all_to_all | solution.py:128
  48.6 28.0 %all_gather.18 = bf16[8,2,24576]{2,1,0:T(2,128)(2,1)S(1)} all-gather(bf16[1,2,24576]{2,1,0:T(2,128)(2,1)S(1)} %convert_element_type.160), channel_id=1, replica_groups=mesh['section'=8,'sht'=64] {'section'}, dimensions={0}, use_global_device_ids=true | all-gather | bytes 884736 | tf_op jit(solution)/shard_map/all_gather | solution.py:131
  76.6 341.6 %while.15 = (s32[]{:T(128)}, bf16[1,2,256,192]{2,3,1,0:T(8,128)(2,1)S(1)}, bf16[8,2,256,192]{2,3,1,0:T(8,128)(2,1)}, f32[8,2,192]{2,1,0:T(2,128)S(1)}, bf16[256,...) while((s32[]{:T(128)}, ...), condition=%wide.region_8.9_spmd, body=%wide.region_3.8_spmd.sunk | while | flops 362300416 | bytes 15677157 | solution.py:193
  77.9 18.4 %all-to-all-start = ((bf16[1,2,128,384]{3,1,0,2:T(2,128)(2,1)}), bf16[1,2,128,384]{3,1,0,2:T(2,128)(2,1)S(1)}, u32[]{:S(2)}, u32[]{:S(2)}) async-start(bf16[1,2,128,384]{3,1,0,2:T(2,128)(2,1)} %copy.107), calls=%async_computation | async-start | bytes 393216 | tf_op jit(solution)/shard_map/while/body/eval_jaxpr/all_to_all | solution.py:148
  97.3 10.0 %all-to-all-done = bf16[1,2,128,384]{3,1,0,2:T(2,128)(2,1)S(1)} async-done(((bf16[1,2,128,384]{3,1,0,2:T(2,128)(2,1)}), bf16[1,2,128,384]{3,1,0,2:T(2,128)(2,1)S(1)}, u32[]{:S(2)}, u32[]{:S(2)}) %all-to-all-start) | async-done | bytes 196640 | tf_op jit(solution)/shard_map/while/body/eval_jaxpr/all_to_all | solution.py:148
  108.8 5.7 %all-to-all-start.1 = ((bf16[1,128,2,384]{3,2,0,1:T(2,128)(2,1)}), bf16[1,128,2,384]{3,2,0,1:T(2,128)(2,1)S(1)}, u32[]{:S(2)}, u32[]{:S(2)}) async-start(bf16[1,128,2,384]{3,2,0,1:T(2,128)(2,1)} %copy.111), calls=%async_computation.1 | async-start | bytes 393216 | tf_op jit(solution)/shard_map/while/body/eval_jaxpr/all_to_all | solution.py:162
  116.0 9.4 %all-to-all-done.1 = bf16[1,128,2,384]{3,2,0,1:T(2,128)(2,1)S(1)} async-done(((bf16[1,128,2,384]{3,2,0,1:T(2,128)(2,1)}), bf16[1,128,2,384]{3,2,0,1:T(2,128)(2,1)S(1)}, u32[]{:S(2)}, u32[]{:S(2)}) %all-to-all-start.1) | async-done | bytes 196640 | tf_op jit(solution)/shard_map/while/body/eval_jaxpr/all_to_all | solution.py:162
  127.3 2.2 fusion.162
  131.8 5.7 %all-to-all-start = ((bf16[1,2,128,384]{3,1,0,2:T(2,128)(2,1)}), bf16[1,2,128,384]{3,1,0,2:T(2,128)(2,1)S(1)}, u32[]{:S(2)}, u32[]{:S(2)}) async-start(bf16[1,2,128,384]{3,1,0,2:T(2,128)(2,1)} %copy.107), calls=%async_computation | async-start | bytes 393216 | tf_op jit(solution)/shard_map/while/body/eval_jaxpr/all_to_all | solution.py:148
  138.4 10.0 %all-to-all-done = bf16[1,2,128,384]{3,1,0,2:T(2,128)(2,1)S(1)} async-done(((bf16[1,2,128,384]{3,1,0,2:T(2,128)(2,1)}), bf16[1,2,128,384]{3,1,0,2:T(2,128)(2,1)S(1)}, u32[]{:S(2)}, u32[]{:S(2)}) %all-to-all-start) | async-done | bytes 196640 | tf_op jit(solution)/shard_map/while/body/eval_jaxpr/all_to_all | solution.py:148
  150.0 5.7 %all-to-all-start.1 = ((bf16[1,128,2,384]{3,2,0,1:T(2,128)(2,1)}), bf16[1,128,2,384]{3,2,0,1:T(2,128)(2,1)S(1)}, u32[]{:S(2)}, u32[]{:S(2)}) async-start(bf16[1,128,2,384]{3,2,0,1:T(2,128)(2,1)} %copy.111), calls=%async_computation.1 | async-start | bytes 393216 | tf_op jit(solution)/shard_map/while/body/eval_jaxpr/all_to_all | solution.py:162
  157.1 9.4 %all-to-all-done.1 = bf16[1,128,2,384]{3,2,0,1:T(2,128)(2,1)S(1)} async-done(((bf16[1,128,2,384]{3,2,0,1:T(2,128)(2,1)}), bf16[1,128,2,384]{3,2,0,1:T(2,128)(2,1)S(1)}, u32[]{:S(2)}, u32[]{:S(2)}) %all-to-all-start.1) | async-done | bytes 196640 | tf_op jit(solution)/shard_map/while/body/eval_jaxpr/all_to_all | solution.py:162
  168.4 2.2 fusion.162
  172.9 5.7 %all-to-all-start = ((bf16[1,2,128,384]{3,1,0,2:T(2,128)(2,1)}), bf16[1,2,128,384]{3,1,0,2:T(2,128)(2,1)S(1)}, u32[]{:S(2)}, u32[]{:S(2)}) async-start(bf16[1,2,128,384]{3,1,0,2:T(2,128)(2,1)} %copy.107), calls=%async_computation | async-start | bytes 393216 | tf_op jit(solution)/shard_map/while/body/eval_jaxpr/all_to_all | solution.py:148
  179.5 10.0 %all-to-all-done = bf16[1,2,128,384]{3,1,0,2:T(2,128)(2,1)S(1)} async-done(((bf16[1,2,128,384]{3,1,0,2:T(2,128)(2,1)}), bf16[1,2,128,384]{3,1,0,2:T(2,128)(2,1)S(1)}, u32[]{:S(2)}, u32[]{:S(2)}) %all-to-all-start) | async-done | bytes 196640 | tf_op jit(solution)/shard_map/while/body/eval_jaxpr/all_to_all | solution.py:148
  191.1 5.7 %all-to-all-start.1 = ((bf16[1,128,2,384]{3,2,0,1:T(2,128)(2,1)}), bf16[1,128,2,384]{3,2,0,1:T(2,128)(2,1)S(1)}, u32[]{:S(2)}, u32[]{:S(2)}) async-start(bf16[1,128,2,384]{3,2,0,1:T(2,128)(2,1)} %copy.111), calls=%async_computation.1 | async-start | bytes 393216 | tf_op jit(solution)/shard_map/while/body/eval_jaxpr/all_to_all | solution.py:162
  198.2 9.4 %all-to-all-done.1 = bf16[1,128,2,384]{3,2,0,1:T(2,128)(2,1)S(1)} async-done(((bf16[1,128,2,384]{3,2,0,1:T(2,128)(2,1)}), bf16[1,128,2,384]{3,2,0,1:T(2,128)(2,1)S(1)}, u32[]{:S(2)}, u32[]{:S(2)}) %all-to-all-start.1) | async-done | bytes 196640 | tf_op jit(solution)/shard_map/while/body/eval_jaxpr/all_to_all | solution.py:162
  209.6 2.2 fusion.162
  214.0 5.7 %all-to-all-start = ((bf16[1,2,128,384]{3,1,0,2:T(2,128)(2,1)}), bf16[1,2,128,384]{3,1,0,2:T(2,128)(2,1)S(1)}, u32[]{:S(2)}, u32[]{:S(2)}) async-start(bf16[1,2,128,384]{3,1,0,2:T(2,128)(2,1)} %copy.107), calls=%async_computation | async-start | bytes 393216 | tf_op jit(solution)/shard_map/while/body/eval_jaxpr/all_to_all | solution.py:148
  220.6 10.0 %all-to-all-done = bf16[1,2,128,384]{3,1,0,2:T(2,128)(2,1)S(1)} async-done(((bf16[1,2,128,384]{3,1,0,2:T(2,128)(2,1)}), bf16[1,2,128,384]{3,1,0,2:T(2,128)(2,1)S(1)}, u32[]{:S(2)}, u32[]{:S(2)}) %all-to-all-start) | async-done | bytes 196640 | tf_op jit(solution)/shard_map/while/body/eval_jaxpr/all_to_all | solution.py:148
  232.2 5.7 %all-to-all-start.1 = ((bf16[1,128,2,384]{3,2,0,1:T(2,128)(2,1)}), bf16[1,128,2,384]{3,2,0,1:T(2,128)(2,1)S(1)}, u32[]{:S(2)}, u32[]{:S(2)}) async-start(bf16[1,128,2,384]{3,2,0,1:T(2,128)(2,1)} %copy.111), calls=%async_computation.1 | async-start | bytes 393216 | tf_op jit(solution)/shard_map/while/body/eval_jaxpr/all_to_all | solution.py:162
  239.3 9.4 %all-to-all-done.1 = bf16[1,128,2,384]{3,2,0,1:T(2,128)(2,1)S(1)} async-done(((bf16[1,128,2,384]{3,2,0,1:T(2,128)(2,1)}), bf16[1,128,2,384]{3,2,0,1:T(2,128)(2,1)S(1)}, u32[]{:S(2)}, u32[]{:S(2)}) %all-to-all-start.1) | async-done | bytes 196640 | tf_op jit(solution)/shard_map/while/body/eval_jaxpr/all_to_all | solution.py:162
  250.7 2.2 fusion.162
  255.1 5.7 %all-to-all-start = ((bf16[1,2,128,384]{3,1,0,2:T(2,128)(2,1)}), bf16[1,2,128,384]{3,1,0,2:T(2,128)(2,1)S(1)}, u32[]{:S(2)}, u32[]{:S(2)}) async-start(bf16[1,2,128,384]{3,1,0,2:T(2,128)(2,1)} %copy.107), calls=%async_computation | async-start | bytes 393216 | tf_op jit(solution)/shard_map/while/body/eval_jaxpr/all_to_all | solution.py:148
  261.7 10.0 %all-to-all-done = bf16[1,2,128,384]{3,1,0,2:T(2,128)(2,1)S(1)} async-done(((bf16[1,2,128,384]{3,1,0,2:T(2,128)(2,1)}), bf16[1,2,128,384]{3,1,0,2:T(2,128)(2,1)S(1)}, u32[]{:S(2)}, u32[]{:S(2)}) %all-to-all-start) | async-done | bytes 196640 | tf_op jit(solution)/shard_map/while/body/eval_jaxpr/all_to_all | solution.py:148
  273.3 5.7 %all-to-all-start.1 = ((bf16[1,128,2,384]{3,2,0,1:T(2,128)(2,1)}), bf16[1,128,2,384]{3,2,0,1:T(2,128)(2,1)S(1)}, u32[]{:S(2)}, u32[]{:S(2)}) async-start(bf16[1,128,2,384]{3,2,0,1:T(2,128)(2,1)} %copy.111), calls=%async_computation.1 | async-start | bytes 393216 | tf_op jit(solution)/shard_map/while/body/eval_jaxpr/all_to_all | solution.py:162
  280.5 9.4 %all-to-all-done.1 = bf16[1,128,2,384]{3,2,0,1:T(2,128)(2,1)S(1)} async-done(((bf16[1,128,2,384]{3,2,0,1:T(2,128)(2,1)}), bf16[1,128,2,384]{3,2,0,1:T(2,128)(2,1)S(1)}, u32[]{:S(2)}, u32[]{:S(2)}) %all-to-all-start.1) | async-done | bytes 196640 | tf_op jit(solution)/shard_map/while/body/eval_jaxpr/all_to_all | solution.py:162
  291.8 2.2 fusion.162
  296.2 5.7 %all-to-all-start = ((bf16[1,2,128,384]{3,1,0,2:T(2,128)(2,1)}), bf16[1,2,128,384]{3,1,0,2:T(2,128)(2,1)S(1)}, u32[]{:S(2)}, u32[]{:S(2)}) async-start(bf16[1,2,128,384]{3,1,0,2:T(2,128)(2,1)} %copy.107), calls=%async_computation | async-start | bytes 393216 | tf_op jit(solution)/shard_map/while/body/eval_jaxpr/all_to_all | solution.py:148
  302.8 10.0 %all-to-all-done = bf16[1,2,128,384]{3,1,0,2:T(2,128)(2,1)S(1)} async-done(((bf16[1,2,128,384]{3,1,0,2:T(2,128)(2,1)}), bf16[1,2,128,384]{3,1,0,2:T(2,128)(2,1)S(1)}, u32[]{:S(2)}, u32[]{:S(2)}) %all-to-all-start) | async-done | bytes 196640 | tf_op jit(solution)/shard_map/while/body/eval_jaxpr/all_to_all | solution.py:148
  314.4 5.7 %all-to-all-start.1 = ((bf16[1,128,2,384]{3,2,0,1:T(2,128)(2,1)}), bf16[1,128,2,384]{3,2,0,1:T(2,128)(2,1)S(1)}, u32[]{:S(2)}, u32[]{:S(2)}) async-start(bf16[1,128,2,384]{3,2,0,1:T(2,128)(2,1)} %copy.111), calls=%async_computation.1 | async-start | bytes 393216 | tf_op jit(solution)/shard_map/while/body/eval_jaxpr/all_to_all | solution.py:162
  321.6 9.4 %all-to-all-done.1 = bf16[1,128,2,384]{3,2,0,1:T(2,128)(2,1)S(1)} async-done(((bf16[1,128,2,384]{3,2,0,1:T(2,128)(2,1)}), bf16[1,128,2,384]{3,2,0,1:T(2,128)(2,1)S(1)}, u32[]{:S(2)}, u32[]{:S(2)}) %all-to-all-start.1) | async-done | bytes 196640 | tf_op jit(solution)/shard_map/while/body/eval_jaxpr/all_to_all | solution.py:162
  332.9 2.2 fusion.162
  337.3 5.7 %all-to-all-start = ((bf16[1,2,128,384]{3,1,0,2:T(2,128)(2,1)}), bf16[1,2,128,384]{3,1,0,2:T(2,128)(2,1)S(1)}, u32[]{:S(2)}, u32[]{:S(2)}) async-start(bf16[1,2,128,384]{3,1,0,2:T(2,128)(2,1)} %copy.107), calls=%async_computation | async-start | bytes 393216 | tf_op jit(solution)/shard_map/while/body/eval_jaxpr/all_to_all | solution.py:148
  343.9 10.0 %all-to-all-done = bf16[1,2,128,384]{3,1,0,2:T(2,128)(2,1)S(1)} async-done(((bf16[1,2,128,384]{3,1,0,2:T(2,128)(2,1)}), bf16[1,2,128,384]{3,1,0,2:T(2,128)(2,1)S(1)}, u32[]{:S(2)}, u32[]{:S(2)}) %all-to-all-start) | async-done | bytes 196640 | tf_op jit(solution)/shard_map/while/body/eval_jaxpr/all_to_all | solution.py:148
  355.5 5.7 %all-to-all-start.1 = ((bf16[1,128,2,384]{3,2,0,1:T(2,128)(2,1)}), bf16[1,128,2,384]{3,2,0,1:T(2,128)(2,1)S(1)}, u32[]{:S(2)}, u32[]{:S(2)}) async-start(bf16[1,128,2,384]{3,2,0,1:T(2,128)(2,1)} %copy.111), calls=%async_computation.1 | async-start | bytes 393216 | tf_op jit(solution)/shard_map/while/body/eval_jaxpr/all_to_all | solution.py:162
  362.7 9.4 %all-to-all-done.1 = bf16[1,128,2,384]{3,2,0,1:T(2,128)(2,1)S(1)} async-done(((bf16[1,128,2,384]{3,2,0,1:T(2,128)(2,1)}), bf16[1,128,2,384]{3,2,0,1:T(2,128)(2,1)S(1)}, u32[]{:S(2)}, u32[]{:S(2)}) %all-to-all-start.1) | async-done | bytes 196640 | tf_op jit(solution)/shard_map/while/body/eval_jaxpr/all_to_all | solution.py:162
  374.0 2.2 fusion.162
  378.4 5.7 %all-to-all-start = ((bf16[1,2,128,384]{3,1,0,2:T(2,128)(2,1)}), bf16[1,2,128,384]{3,1,0,2:T(2,128)(2,1)S(1)}, u32[]{:S(2)}, u32[]{:S(2)}) async-start(bf16[1,2,128,384]{3,1,0,2:T(2,128)(2,1)} %copy.107), calls=%async_computation | async-start | bytes 393216 | tf_op jit(solution)/shard_map/while/body/eval_jaxpr/all_to_all | solution.py:148
  385.0 10.0 %all-to-all-done = bf16[1,2,128,384]{3,1,0,2:T(2,128)(2,1)S(1)} async-done(((bf16[1,2,128,384]{3,1,0,2:T(2,128)(2,1)}), bf16[1,2,128,384]{3,1,0,2:T(2,128)(2,1)S(1)}, u32[]{:S(2)}, u32[]{:S(2)}) %all-to-all-start) | async-done | bytes 196640 | tf_op jit(solution)/shard_map/while/body/eval_jaxpr/all_to_all | solution.py:148
  396.6 5.7 %all-to-all-start.1 = ((bf16[1,128,2,384]{3,2,0,1:T(2,128)(2,1)}), bf16[1,128,2,384]{3,2,0,1:T(2,128)(2,1)S(1)}, u32[]{:S(2)}, u32[]{:S(2)}) async-start(bf16[1,128,2,384]{3,2,0,1:T(2,128)(2,1)} %copy.111), calls=%async_computation.1 | async-start | bytes 393216 | tf_op jit(solution)/shard_map/while/body/eval_jaxpr/all_to_all | solution.py:162
  403.8 9.4 %all-to-all-done.1 = bf16[1,128,2,384]{3,2,0,1:T(2,128)(2,1)S(1)} async-done(((bf16[1,128,2,384]{3,2,0,1:T(2,128)(2,1)}), bf16[1,128,2,384]{3,2,0,1:T(2,128)(2,1)S(1)}, u32[]{:S(2)}, u32[]{:S(2)}) %all-to-all-start.1) | async-done | bytes 196640 | tf_op jit(solution)/shard_map/while/body/eval_jaxpr/all_to_all | solution.py:162
  415.1 2.2 fusion.162
  418.2 44.6 %all_to_all.66 = bf16[8,2,256,192]{2,3,1,0:T(8,128)(2,1)S(1)} all-to-all(bf16[8,2,256,192]{2,3,1,0:T(8,128)(2,1)} %get-tuple-element.174), channel_id=1, replica_groups=mesh['section'=8,'sht'=64] {'section'}, dimensions={0} | all-to-all | bytes 3145728 | tf_op jit(solution)/shard_map/all_to_all | solution.py:194
  463.6 3.4 reshape.623
  (319 shorter events, 73.3 us)
Async XLA Ops:
  6.5 70.1 %all-gather.5.cloned.1.call-start = ((), (), s32[]{:S(2)}) async-start(), calls=%async_computation.4 | async-start | bytes 3538944 | tf_op jit(solution)/shard_map/all_gather | solution.py:132
  6.5 10.5 %copy-start.1 = (f32[1,2,24576]{2,1,0:T(2,128)S(1)}, f32[1,2,24576]{2,1,0:T(2,128)}, u32[]{:S(2)}) copy-start(f32[1,2,24576]{2,1,0:T(2,128)} %param.13) | copy-start | bytes 589828
  8.5 8.6 %copy-start.2 = (bf16[2,256,24]{1,2,0:T(8,128)(2,1)S(1)}, bf16[2,256,24]{1,2,0:T(8,128)(2,1)}, u32[]{:S(2)}) copy-start(bf16[2,256,24]{1,2,0:T(8,128)(2,1)} %param.10) | copy-start | bytes 73732
  8.5 8.6 %copy-start = (bf16[6,2,256,24]{2,3,1,0:T(8,128)(2,1)S(1)}, bf16[6,2,256,24]{2,3,1,0:T(8,128)(2,1)}, u32[]{:S(2)}) copy-start(bf16[6,2,256,24]{2,3,1,0:T(8,128)(2,1)} %param.11) | copy-start | bytes 442372
  9.4 8.6 %copy-start.3 = (f32[1,192]{1,0:T(1,128)S(1)}, f32[1,192]{1,0:T(1,128)}, u32[]{:S(2)}) copy-start(f32[1,192]{1,0:T(1,128)} %param.15) | copy-start | bytes 2308
  9.4 8.6 %copy-start.4 = (f32[1,192]{1,0:T(1,128)S(1)}, f32[1,192]{1,0:T(1,128)}, u32[]{:S(2)}) copy-start(f32[1,192]{1,0:T(1,128)} %param.12) | copy-start | bytes 2308
  43.7 32.9 %all-to-all-start.2 = ((bf16[8,2,256,24]{2,3,1,0:T(8,128)(2,1)}), bf16[8,2,256,24]{2,3,1,0:T(8,128)(2,1)S(1)}, u32[]{:S(2)}, u32[]{:S(2)}) async-start(bf16[8,2,256,24]{2,3,1,0:T(8,128)(2,1)} %pad.4), calls=%async_computation.2 | async-start | bytes 393216 | tf_op jit(solution)/shard_map/all_to_all | solution.py:128
  77.9 29.4 %all-to-all-start = ((bf16[1,2,128,384]{3,1,0,2:T(2,128)(2,1)}), bf16[1,2,128,384]{3,1,0,2:T(2,128)(2,1)S(1)}, u32[]{:S(2)}, u32[]{:S(2)}) async-start(bf16[1,2,128,384]{3,1,0,2:T(2,128)(2,1)} %copy.107), calls=%async_computation | async-start | bytes 393216 | tf_op jit(solution)/shard_map/while/body/eval_jaxpr/all_to_all | solution.py:148
  108.8 16.6 %all-to-all-start.1 = ((bf16[1,128,2,384]{3,2,0,1:T(2,128)(2,1)}), bf16[1,128,2,384]{3,2,0,1:T(2,128)(2,1)S(1)}, u32[]{:S(2)}, u32[]{:S(2)}) async-start(bf16[1,128,2,384]{3,2,0,1:T(2,128)(2,1)} %copy.111), calls=%async_computation.1 | async-start | bytes 393216 | tf_op jit(solution)/shard_map/while/body/eval_jaxpr/all_to_all | solution.py:162
  131.8 16.6 %all-to-all-start = ((bf16[1,2,128,384]{3,1,0,2:T(2,128)(2,1)}), bf16[1,2,128,384]{3,1,0,2:T(2,128)(2,1)S(1)}, u32[]{:S(2)}, u32[]{:S(2)}) async-start(bf16[1,2,128,384]{3,1,0,2:T(2,128)(2,1)} %copy.107), calls=%async_computation | async-start | bytes 393216 | tf_op jit(solution)/shard_map/while/body/eval_jaxpr/all_to_all | solution.py:148
  150.0 16.6 %all-to-all-start.1 = ((bf16[1,128,2,384]{3,2,0,1:T(2,128)(2,1)}), bf16[1,128,2,384]{3,2,0,1:T(2,128)(2,1)S(1)}, u32[]{:S(2)}, u32[]{:S(2)}) async-start(bf16[1,128,2,384]{3,2,0,1:T(2,128)(2,1)} %copy.111), calls=%async_computation.1 | async-start | bytes 393216 | tf_op jit(solution)/shard_map/while/body/eval_jaxpr/all_to_all | solution.py:162
  172.9 16.6 %all-to-all-start = ((bf16[1,2,128,384]{3,1,0,2:T(2,128)(2,1)}), bf16[1,2,128,384]{3,1,0,2:T(2,128)(2,1)S(1)}, u32[]{:S(2)}, u32[]{:S(2)}) async-start(bf16[1,2,128,384]{3,1,0,2:T(2,128)(2,1)} %copy.107), calls=%async_computation | async-start | bytes 393216 | tf_op jit(solution)/shard_map/while/body/eval_jaxpr/all_to_all | solution.py:148
  191.1 16.6 %all-to-all-start.1 = ((bf16[1,128,2,384]{3,2,0,1:T(2,128)(2,1)}), bf16[1,128,2,384]{3,2,0,1:T(2,128)(2,1)S(1)}, u32[]{:S(2)}, u32[]{:S(2)}) async-start(bf16[1,128,2,384]{3,2,0,1:T(2,128)(2,1)} %copy.111), calls=%async_computation.1 | async-start | bytes 393216 | tf_op jit(solution)/shard_map/while/body/eval_jaxpr/all_to_all | solution.py:162
  214.0 16.6 %all-to-all-start = ((bf16[1,2,128,384]{3,1,0,2:T(2,128)(2,1)}), bf16[1,2,128,384]{3,1,0,2:T(2,128)(2,1)S(1)}, u32[]{:S(2)}, u32[]{:S(2)}) async-start(bf16[1,2,128,384]{3,1,0,2:T(2,128)(2,1)} %copy.107), calls=%async_computation | async-start | bytes 393216 | tf_op jit(solution)/shard_map/while/body/eval_jaxpr/all_to_all | solution.py:148
  232.2 16.6 %all-to-all-start.1 = ((bf16[1,128,2,384]{3,2,0,1:T(2,128)(2,1)}), bf16[1,128,2,384]{3,2,0,1:T(2,128)(2,1)S(1)}, u32[]{:S(2)}, u32[]{:S(2)}) async-start(bf16[1,128,2,384]{3,2,0,1:T(2,128)(2,1)} %copy.111), calls=%async_computation.1 | async-start | bytes 393216 | tf_op jit(solution)/shard_map/while/body/eval_jaxpr/all_to_all | solution.py:162
  255.1 16.6 %all-to-all-start = ((bf16[1,2,128,384]{3,1,0,2:T(2,128)(2,1)}), bf16[1,2,128,384]{3,1,0,2:T(2,128)(2,1)S(1)}, u32[]{:S(2)}, u32[]{:S(2)}) async-start(bf16[1,2,128,384]{3,1,0,2:T(2,128)(2,1)} %copy.107), calls=%async_computation | async-start | bytes 393216 | tf_op jit(solution)/shard_map/while/body/eval_jaxpr/all_to_all | solution.py:148
  273.3 16.6 %all-to-all-start.1 = ((bf16[1,128,2,384]{3,2,0,1:T(2,128)(2,1)}), bf16[1,128,2,384]{3,2,0,1:T(2,128)(2,1)S(1)}, u32[]{:S(2)}, u32[]{:S(2)}) async-start(bf16[1,128,2,384]{3,2,0,1:T(2,128)(2,1)} %copy.111), calls=%async_computation.1 | async-start | bytes 393216 | tf_op jit(solution)/shard_map/while/body/eval_jaxpr/all_to_all | solution.py:162
  296.2 16.6 %all-to-all-start = ((bf16[1,2,128,384]{3,1,0,2:T(2,128)(2,1)}), bf16[1,2,128,384]{3,1,0,2:T(2,128)(2,1)S(1)}, u32[]{:S(2)}, u32[]{:S(2)}) async-start(bf16[1,2,128,384]{3,1,0,2:T(2,128)(2,1)} %copy.107), calls=%async_computation | async-start | bytes 393216 | tf_op jit(solution)/shard_map/while/body/eval_jaxpr/all_to_all | solution.py:148
  314.4 16.6 %all-to-all-start.1 = ((bf16[1,128,2,384]{3,2,0,1:T(2,128)(2,1)}), bf16[1,128,2,384]{3,2,0,1:T(2,128)(2,1)S(1)}, u32[]{:S(2)}, u32[]{:S(2)}) async-start(bf16[1,128,2,384]{3,2,0,1:T(2,128)(2,1)} %copy.111), calls=%async_computation.1 | async-start | bytes 393216 | tf_op jit(solution)/shard_map/while/body/eval_jaxpr/all_to_all | solution.py:162
  337.3 16.6 %all-to-all-start = ((bf16[1,2,128,384]{3,1,0,2:T(2,128)(2,1)}), bf16[1,2,128,384]{3,1,0,2:T(2,128)(2,1)S(1)}, u32[]{:S(2)}, u32[]{:S(2)}) async-start(bf16[1,2,128,384]{3,1,0,2:T(2,128)(2,1)} %copy.107), calls=%async_computation | async-start | bytes 393216 | tf_op jit(solution)/shard_map/while/body/eval_jaxpr/all_to_all | solution.py:148
  355.5 16.6 %all-to-all-start.1 = ((bf16[1,128,2,384]{3,2,0,1:T(2,128)(2,1)}), bf16[1,128,2,384]{3,2,0,1:T(2,128)(2,1)S(1)}, u32[]{:S(2)}, u32[]{:S(2)}) async-start(bf16[1,128,2,384]{3,2,0,1:T(2,128)(2,1)} %copy.111), calls=%async_computation.1 | async-start | bytes 393216 | tf_op jit(solution)/shard_map/while/body/eval_jaxpr/all_to_all | solution.py:162
  378.4 16.6 %all-to-all-start = ((bf16[1,2,128,384]{3,1,0,2:T(2,128)(2,1)}), bf16[1,2,128,384]{3,1,0,2:T(2,128)(2,1)S(1)}, u32[]{:S(2)}, u32[]{:S(2)}) async-start(bf16[1,2,128,384]{3,1,0,2:T(2,128)(2,1)} %copy.107), calls=%async_computation | async-start | bytes 393216 | tf_op jit(solution)/shard_map/while/body/eval_jaxpr/all_to_all | solution.py:148
  396.6 16.6 %all-to-all-start.1 = ((bf16[1,128,2,384]{3,2,0,1:T(2,128)(2,1)}), bf16[1,128,2,384]{3,2,0,1:T(2,128)(2,1)S(1)}, u32[]{:S(2)}, u32[]{:S(2)}) async-start(bf16[1,128,2,384]{3,2,0,1:T(2,128)(2,1)} %copy.111), calls=%async_computation.1 | async-start | bytes 393216 | tf_op jit(solution)/shard_map/while/body/eval_jaxpr/all_to_all | solution.py:162
Sparse Core Ops, SparseCore 0:
  9.4 62.0 all-gather.4

commit v2 on v1

v2 whole, which is shorter than its diff:
```python
import math

import jax
import jax.numpy as jnp
import numpy as np
from jax import lax
from jax.experimental import pallas as pl
from jax.experimental.pallas import tpu as pltpu
from jax.sharding import PartitionSpec as P

C = 192
HID = 384
NLAT = 128
NLON = 256
LMAX = 128
MMAX = 128
MEMBERS = 6
SECTIONS = 8
SHT = 64
IDLE = 2
PAD = 256
HALF = 128
MESH = pl.DeviceIdType.MESH
BF = jnp.bfloat16
F32 = jnp.float32


def longitude_tables():
    order = np.concatenate([np.arange(0, NLON, 2), np.arange(1, NLON, 2)])
    waves = np.arange(MMAX)
    phase = (waves[:, None] * order[None, :] % NLON).astype(np.float32) * np.float32(
        2.0 * math.pi / NLON
    )
    cosines = np.cos(phase)
    sines = np.sin(phase)
    forward = np.stack([cosines, -sines])
    factor = np.where(waves == 0, 1.0, 2.0).astype(np.float32)
    inverse = np.concatenate([cosines.T * factor, -sines.T * factor], axis=1)
    return jnp.asarray(forward, BF), jnp.asarray(inverse, BF)


def latitude_rows():
    lane = np.arange(2 * NLAT)
    colatitude = (math.pi * (lane // 2 + 0.5) / NLAT).astype(np.float32)
    sine = np.sin(colatitude)
    rows = np.zeros((8, 2 * NLAT), np.float32)
    rows[0] = np.cos(colatitude)
    rows[1] = sine
    rows[2] = np.log(sine)
    rows[3] = sine * (2.0 * math.pi / NLON) * (math.pi / NLAT)
    rows[4] = lane % 2
    return jnp.asarray(rows)


def gelu(x):
    return 0.5 * x * (1.0 + lax.erf(x * math.sqrt(0.5)))


def lane_of(shape):
    return lax.broadcasted_iota(jnp.int32, shape, len(shape) - 1)


def layer_norm(values, gain_row):
    average = jnp.sum(values, axis=1, keepdims=True) * (1.0 / C)
    centred = jnp.where(lane_of(values.shape) < C, values - average, 0.0)
    variance = jnp.sum(centred * centred, axis=1, keepdims=True) * (1.0 / C)
    return centred * lax.rsqrt(variance + 1e-05) * gain_row


def dot(a, b):
    return jnp.dot(a, b, preferred_element_type=F32)


def build_legendre(me, rows_ref, lower, upper, first, table, forward_table, inverse_table):
    cosine = rows_ref[0:1, :]
    parity = rows_ref[4:5, :]
    order = parity + (2 * me).astype(F32)
    shape = (LMAX, 2 * NLAT)
    degree = lax.broadcasted_iota(jnp.int32, shape, 0).astype(F32)
    step = degree + 1.0
    terms = jnp.where(step <= order, 0.5 * jnp.log((2.0 * step + 1.0) / (2.0 * step)), 0.0)
    picked = jnp.sum(terms, axis=0, keepdims=True)
    diagonal = jnp.exp(picked + order * rows_ref[2:3, :]) * math.sqrt(0.25 / math.pi)
    lower[...] = jnp.sqrt(
        jnp.maximum(4.0 * degree * degree - 1.0, 0.0)
        / jnp.maximum(degree * degree - order * order, 1.0)
    )
    shifted = degree - 1.0
    upper[...] = jnp.sqrt(
        jnp.maximum(shifted * shifted - order * order, 0.0)
        / jnp.maximum(4.0 * shifted * shifted - 1.0, 1.0)
    )
    first[...] = jnp.where(degree == order, diagonal, 0.0)

    def advance(row, carry):
        latest, earlier = carry
        at = pl.ds(row, 1)
        current = lower[at, :] * (cosine * latest - upper[at, :] * earlier) + first[at, :]
        table[at, :] = current
        return (current, latest)

    zero = cosine * 0.0
    lax.fori_loop(0, LMAX, advance, (zero, zero), unroll=8)
    plain = table[...]
    weighted = plain * rows_ref[3:4, :]
    even = jnp.broadcast_to(parity, shape) < 0.5
    forward_table[0:LMAX, :] = jnp.where(even, weighted, 0.0).astype(BF)
    forward_table[LMAX:, :] = jnp.where(even, 0.0, weighted).astype(BF)
    inverse_table[:, 0:LMAX] = jnp.where(even, plain, 0.0).T.astype(BF)
    inverse_table[:, LMAX:] = jnp.where(even, 0.0, plain).T.astype(BF)


def kernel(
    state_in, gains_in, filter_in, matrix_in, fourier, inverse_fourier, rows,
    out,
    state, normed, skipped, send_one, send_two, recv_one, recv_two,
    gains, filters, matrices, lower, upper, first, table, legendre, legendre_back, leaving,
    sent_one, sent_two, got_one, got_two, weight_sent, weight_got,
    share_sent, share_got, out_sent, out_got, pace,
):
    section = lax.axis_index("section")
    me = lax.axis_index("sht")
    core = lax.rem(me, 2)
    sibling = me + 1 - 2 * core

    barrier = pltpu.get_barrier_semaphore()

    def greet(t, carry):
        pl.semaphore_signal(
            barrier, inc=1, device_id={"sht": lax.rem(me + t, SHT)}, device_id_type=MESH
        )
        return carry

    def greet_column(t, carry):
        pl.semaphore_signal(
            barrier, inc=1, device_id={"section": lax.rem(section + t, SECTIONS)},
            device_id_type=MESH,
        )
        return carry

    lax.fori_loop(1, SHT, greet, 0)
    lax.fori_loop(1, SECTIONS, greet_column, 0)

    matrices[:, C:, :] = jnp.zeros((SECTIONS, PAD - C, 1024), BF)
    matrices[section, 0:C, :] = matrix_in[...]
    filters[section] = filter_in[...]
    gains[section] = gains_in[...]
    build_legendre(me, rows, lower, upper, first, table, legendre, legendre_back)
    state[...] = state_in[...]

    pl.semaphore_wait(barrier, SHT - 1 + SECTIONS - 1)

    filter_half = pl.ds(pl.multiple_of(core * (LMAX // 2), LMAX // 2), LMAX // 2)
    matrix_half = pl.ds(pl.multiple_of(core * (C // 2), C // 2), C // 2)

    def weight_copies(target):
        refs = [
            (gains_in, gains.at[section]),
            (filter_in.at[filter_half], filters.at[section, filter_half]),
            (matrix_in.at[matrix_half], matrices.at[section, matrix_half]),
        ]
        return [
            pltpu.make_async_remote_copy(
                src_ref=source, dst_ref=target_ref, send_sem=weight_sent.at[i, target],
                recv_sem=weight_got.at[i, section], device_id={"section": target},
                device_id_type=MESH,
            )
            for i, (source, target_ref) in enumerate(refs)
        ]

    def send_weights():
        for i in range(3):
            for target in range(IDLE, SECTIONS):

                @pl.when(section != target)
                def _():
                    weight_copies(target)[i].start()

    def arrived(i, block):
        refs = [
            gains.at[block],
            filters.at[block, filter_half],
            matrices.at[block, matrix_half],
        ]
        pltpu.make_async_copy(refs[i], refs[i], weight_got.at[i, block]).wait()

    def share(i, block):
        ref = filters.at[block, filter_half] if i == 0 else matrices.at[block, matrix_half]
        return pltpu.make_async_remote_copy(
            src_ref=ref, dst_ref=ref, send_sem=share_sent.at[i], recv_sem=share_got.at[i, block],
            device_id={"sht": sibling}, device_id_type=MESH,
        )

    @pl.when(section == 0)
    def _():
        send_weights()

    @pl.when(section == 1)
    def _():
        pl.semaphore_wait(pace, 1)
        send_weights()

    def exchange(send, recv, sent, got):
        recv[me] = send[me]

        def one(t, carry):
            to = lax.rem(me + t, SHT)
            pltpu.make_async_remote_copy(
                src_ref=send.at[to], dst_ref=recv.at[me], send_sem=sent, recv_sem=got,
                device_id={"sht": to}, device_id_type=MESH,
            ).start()
            return carry

        lax.fori_loop(1, SHT, one, 0)

    def wait_all(buffer, semaphore):
        ref = buffer.at[pl.ds(0, SHT - 1)]
        pltpu.make_async_copy(ref, ref, semaphore).wait()

    def out_copy(lat, slot, member, block):
        return pltpu.make_async_remote_copy(
            src_ref=leaving.at[slot, lat], dst_ref=out.at[member, lat],
            send_sem=out_sent.at[slot, lat], recv_sem=out_got.at[member, lat],
            device_id={"section": block}, device_id_type=MESH,
        )

    def own_copy(lat, slot, member):
        return pltpu.make_async_copy(
            leaving.at[slot, lat], out.at[member, lat], out_sent.at[slot, lat]
        )

    def wait_left(lat, slot):
        ref = leaving.at[slot, lat]
        pltpu.make_async_copy(ref, ref, out_sent.at[slot, lat]).wait()

    low = lane_of((HALF, HALF)) < HALF // 2
    low_all = lane_of((NLON, HALF)) < HALF // 2

    def step(block, carry):
        away = section != block

        @pl.when(section == block + 2)
        def _():
            send_weights()

        @pl.when(away)
        def _():
            arrived(0, block)

        for lat in range(2):
            wide = layer_norm(state[lat].astype(F32), gains[block, 0:1, :])
            narrow = wide.astype(BF)
            normed[lat] = narrow
            turned = pltpu.roll(wide[:, HALF:], HALF // 2, 1).astype(BF)
            real = dot(fourier[0], narrow)
            imag = dot(fourier[1], jnp.concatenate([narrow[:, :HALF], turned], axis=1))
            spectrum = jnp.concatenate(
                [real[:, :HALF], imag[:, :HALF], real[:, HALF:] + imag[:, HALF:]], axis=1
            ).astype(BF)
            send_one[:, 2 * lat : 2 * lat + 2, :] = spectrum.reshape(SHT, 2, 2 * C)
        exchange(send_one, recv_one, sent_one, got_one)

        @pl.when(away)
        def _():
            arrived(1, block)
            share(0, block).start()

        wait_all(recv_one, got_one)
        coeffs = dot(legendre[...], recv_one[...].reshape(2 * NLAT, 2 * C))

        @pl.when(away)
        def _():
            share(0, block).wait()

        gain = filters[block].astype(F32)
        gain_real, gain_imag = gain[:, :HALF], gain[:, HALF : 2 * HALF]
        gain_rest = gain[:, 2 * HALF :]
        gain_turned = pltpu.roll(gain_rest, HALF // 2, 1)
        gain_straight = jnp.where(low, gain_rest, gain_turned)
        gain_cross = jnp.where(low, -gain_turned, gain_rest)
        parts = []
        for order in range(2):
            part = coeffs[order * LMAX : (order + 1) * LMAX]
            real, imag, rest = part[:, :HALF], part[:, HALF : 2 * HALF], part[:, 2 * HALF :]
            parts.append(
                jnp.concatenate(
                    [
                        real * gain_real - imag * gain_imag,
                        real * gain_imag + imag * gain_real,
                        rest * gain_straight + pltpu.roll(rest, HALF // 2, 1) * gain_cross,
                    ],
                    axis=1,
                )
            )
        filtered = jnp.concatenate(parts, axis=0).astype(BF)
        returned = dot(legendre_back[...], filtered).astype(BF)

        wait_all(send_one, sent_one)

        send_two[...] = returned.reshape(SHT, 4, 2 * C)
        exchange(send_two, recv_two, sent_two, got_two)

        @pl.when(away)
        def _():
            arrived(2, block)
            copy = share(1, block)
            copy.start()
            copy.wait()

        @pl.when(jnp.logical_and(block == 0, section == 4))
        def _():
            pl.semaphore_signal(pace, inc=1, device_id={"section": 1}, device_id_type=MESH)

        skip = matrices[block, :, 0:PAD]
        into = matrices[block, :, PAD : PAD + HID]
        back = matrices[block, :, PAD + HID :]
        for lat in range(2):
            skipped[lat] = dot(normed[lat], skip)

        wait_all(recv_two, got_two)
        slot = lax.rem(block, 2)
        for lat in range(2):
            waves = recv_two[:, 2 * lat : 2 * lat + 2, :].reshape(MMAX, 2 * C)
            rest = waves[:, 2 * HALF :].astype(F32)
            top = jnp.where(low, rest, 0.0).astype(BF)
            bottom = jnp.where(low, pltpu.roll(rest, HALF // 2, 1), 0.0).astype(BF)
            stacked = jnp.concatenate(
                [
                    jnp.concatenate([waves[:, :HALF], top], axis=1),
                    jnp.concatenate([waves[:, HALF : 2 * HALF], bottom], axis=1),
                ],
                axis=0,
            )
            activated = gelu(dot(inverse_fourier[...], stacked) + skipped[lat])
            second = layer_norm(activated, gains[block, 1:2, :]).astype(BF)
            hidden = gelu(dot(second, into)).astype(BF)
            update = lax.dot_general(
                hidden, back, (((1,), (1,)), ((), ())), preferred_element_type=F32
            )
            result = state[lat].astype(F32) + update
            state[lat] = result.astype(BF)

            @pl.when(block >= 2)
            def _():
                wait_left(lat, slot)

            odd = pltpu.roll(result[NLON // 2 :, :HALF], HALF // 2, 1)
            odd_rest = pltpu.roll(result[NLON // 2 :, HALF:], HALF // 2, 1)
            leaving[slot, lat] = jnp.concatenate(
                [
                    result[: NLON // 2, :HALF],
                    jnp.where(low, result[: NLON // 2, HALF:], odd),
                    jnp.where(low, odd, odd_rest),
                ],
                axis=1,
            ).astype(BF)

            @pl.when(away)
            def _():
                out_copy(lat, slot, section - IDLE, block).start()

            @pl.when(jnp.logical_not(away))
            def _():
                own_copy(lat, slot, section - IDLE).start()

        wait_all(send_two, sent_two)
        return carry

    @pl.when(section >= IDLE)
    def _():
        lax.fori_loop(0, SECTIONS, step, 0)
        for slot in range(2):
            for lat in range(2):
                wait_left(lat, slot)

    for target in range(IDLE, SECTIONS):

        @pl.when(section != target)
        def _():
            for copy in weight_copies(target):
                copy.wait_send()

    for member in range(MEMBERS):

        @pl.when(section != member + IDLE)
        def _():
            for lat in range(2):
                ref = out.at[member, lat]
                pltpu.make_async_copy(ref, ref, out_got.at[member, lat]).wait()


def per_device(
    analysis, perturbations, gain_first, spectral_gain, skip_weight, gain_second, mlp_in, mlp_out
):
    wide = perturbations.astype(F32)
    average = jnp.mean(wide, axis=0, keepdims=True)
    members = (analysis.astype(F32)[None] + wide - average).astype(BF)
    members = jnp.pad(members, ((IDLE, 0), (0, 0), (0, 0), (0, 0)))
    slices = lax.all_to_all(members, "section", split_axis=0, concat_axis=0, tiled=True)
    lats = slices.shape[1]
    begin = slices.reshape(SECTIONS, lats, NLON // 2, 2, C // SECTIONS)
    begin = jnp.transpose(begin, (1, 3, 2, 0, 4)).reshape(lats, NLON, C)
    begin = jnp.pad(begin, ((0, 0), (0, 0), (0, PAD - C)))

    gains = jnp.pad(
        jnp.concatenate([gain_first, gain_second], axis=0), ((0, 6), (0, PAD - C))
    )
    g = spectral_gain[0].astype(BF).reshape(2, LMAX, C)
    filters = jnp.concatenate([g[0, :, :HALF], g[1, :, :HALF], g[0, :, HALF:], g[1, :, HALF:]], axis=1)
    matrices = jnp.concatenate(
        [jnp.pad(skip_weight[0], ((0, 0), (0, PAD - C))), mlp_in[0], mlp_out[0]], axis=1
    )
    forward, inverse = longitude_tables()
    vmem = pl.BlockSpec(memory_space=pltpu.VMEM)
    out = pl.pallas_call(
        kernel,
        out_shape=jax.ShapeDtypeStruct((MEMBERS, lats, NLON // 2, 2 * C), BF),
        in_specs=[vmem] * 7,
        out_specs=pl.BlockSpec(memory_space=pl.ANY),
        scratch_shapes=[
            pltpu.VMEM((2, NLON, PAD), BF),
            pltpu.VMEM((2, NLON, PAD), BF),
            pltpu.VMEM((2, NLON, PAD), F32),
            pltpu.VMEM((SHT, 4, 2 * C), BF),
            pltpu.VMEM((SHT, 4, 2 * C), BF),
            pltpu.VMEM((SHT, 4, 2 * C), BF),
            pltpu.VMEM((SHT, 4, 2 * C), BF),
            pltpu.VMEM((SECTIONS, 8, PAD), F32),
            pltpu.VMEM((SECTIONS, LMAX, 2 * C), BF),
            pltpu.VMEM((SECTIONS, PAD, 1024), BF),
            pltpu.VMEM((LMAX, 2 * NLAT), F32),
            pltpu.VMEM((LMAX, 2 * NLAT), F32),
            pltpu.VMEM((LMAX, 2 * NLAT), F32),
            pltpu.VMEM((LMAX, 2 * NLAT), F32),
            pltpu.VMEM((2 * LMAX, 2 * NLAT), BF),
            pltpu.VMEM((2 * NLAT, 2 * LMAX), BF),
            pltpu.VMEM((2, 2, NLON // 2, 2 * C), BF),
            pltpu.SemaphoreType.DMA,
            pltpu.SemaphoreType.DMA,
            pltpu.SemaphoreType.DMA,
            pltpu.SemaphoreType.DMA,
            pltpu.SemaphoreType.DMA((3, SECTIONS)),
            pltpu.SemaphoreType.DMA((3, SECTIONS)),
            pltpu.SemaphoreType.DMA((2,)),
            pltpu.SemaphoreType.DMA((2, SECTIONS)),
            pltpu.SemaphoreType.DMA((2, 2)),
            pltpu.SemaphoreType.DMA((MEMBERS, 2)),
            pltpu.SemaphoreType.REGULAR,
        ],
        compiler_params=pltpu.CompilerParams(
            collective_id=0, has_side_effects=True, vmem_limit_bytes=40 * 1024 * 1024
        ),
    )(begin, gains, filters, matrices, forward, inverse, latitude_rows())
    return out.reshape(1, MEMBERS, lats, NLON * C)


def solution(mesh):
    return jax.shard_map(
        per_device,
        mesh=mesh,
        in_specs=(
            P("sht", None, "section"),
            P(None, "sht", None, "section"),
            P("section", None),
            P("section", None, None),
            P("section", None, None),
            P("section", None),
            P("section", None, None),
            P("section", None, None),
        ),
        out_specs=P("section", None, "sht", None),
        check_vma=False,
    )
```

time: 475 us -> 216 us (0.45)
  the two profiles are of different devices: /device:TPU:1 before, /device:TPU:496 now
where the time goes in v2:
time: 216 us
  Pallas kernels  198 us (92%)
  waiting for transfers between devices  5.77 us (3%)
  starting transfers between devices  4.51 us (2%)
  local copies, waits for them, and re-layouts  4.41 us (2%)
  other arithmetic  2.95 us (1%)
    pallas_call x1, Pallas kernels, per_device(): pl.pallas_call(kernel, out_shape=jax.ShapeDtypeStruct((MEMBERS, lats, NLO...  198 us
    all_to_all x1, waiting for transfers between devices, per_device(): lax.all_to_all(members, 'section', split_axis=0, concat_axis=0, tiled=True)  5.77 us
    all_to_all x1, starting transfers between devices, per_device(): lax.all_to_all(members, 'section', split_axis=0, concat_axis=0, tiled=True)  4.51 us
  transfers between devices with their start and end apart: 1, of which 1 were waited for; matrix products, arithmetic and copies ran while one was open for 0% of the time, Pallas kernels for 0%

profile of v2, /device:TPU:496, one launch (start us, length us, event | category | flops | bytes accessed | tf_op | source)
XLA Modules:
  0.0 215.8 jit_solution(14081026581080293444)
XLA Ops:
  0.0 0.0 copy-start.3
  0.0 0.0 copy-start.7
  0.0 0.0 copy-start.8
  0.0 0.8 convert_element_type.24
  0.8 0.9 convert_reduce_fusion
  1.7 0.0 copy-start.4
  1.7 0.0 copy-start.5
  1.8 0.0 copy-start.6
  1.8 1.0 fusion.4
  2.8 0.7 pad.16
  3.5 4.5 %all-to-all-start = ((bf16[8,2,256,24]{2,3,1,0:T(8,128)(2,1)}), bf16[8,2,256,24]{2,3,1,0:T(8,128)(2,1)S(1)}, u32[]{:S(2)}, u32[]{:S(2)}) async-start(bf16[8,2,256,24]{2,3,1,0:T(8,128)(2,1)} %pad.16), calls=%async_computation | async-start | bytes 393216 | tf_op jit(solution)/shard_map/all_to_all | solution.py:399
  8.0 0.0 copy-done.3
  8.0 0.1 convert_element_type.27
  8.1 0.1 convert_element_type.28
  8.3 0.0 copy-done.7
  8.3 0.0 copy-done.8
  8.3 0.1 pad_maximum_fusion.filter_in
  8.4 0.0 copy-done.4
  8.4 0.0 copy-done.5
  8.4 0.0 copy-done.6
  8.5 5.8 %all-to-all-done = bf16[8,2,256,24]{2,3,1,0:T(8,128)(2,1)S(1)} async-done(((bf16[8,2,256,24]{2,3,1,0:T(8,128)(2,1)}), bf16[8,2,256,24]{2,3,1,0:T(8,128)(2,1)S(1)}, u32[]{:S(2)}, u32[]{:S(2)}) %all-to-all-start) | async-done | bytes 196640 | tf_op jit(solution)/shard_map/all_to_all | solution.py:399
  14.2 0.5 copy.13
  14.8 0.0 copy-start
  14.8 0.0 copy-start.1
  14.8 0.0 copy-start.2
  14.8 0.9 copy.14
  15.8 0.1 reshape.18
  15.9 0.1 copy.15
  16.1 0.0 copy-done
  16.1 0.0 copy-done.1
  16.1 0.0 copy-done.2
  16.1 198.0 %shard_map.109 = bf16[6,2,128,384]{3,2,1,0:T(8,128)(2,1)S(1)} custom-call(bf16[2,256,256]{2,1,0:T(8,128)(2,1)S(1)} %pad.17.state_in, f32[8,256]{1,0:T(8,128)S(1)} %select_maximum_fusion.gains_in, bf16[128,384]{1,0:T(8,128)(2,1)S(1)} %pad_maximum_fusion.filter_in, bf16[192,1024]{1,0:T(8,128)(2,1)S(1)} %fusion.2.matrix_in, bf16[2,128,256]{2,1,0:T(8,128)(2,1)S(1)} %copy-done.1, ...), custom_call_target="tpu_custom_call" | custom-call | tf_op jit(solution)/shard_map/pallas_call | solution.py:415
  214.1 1.7 reshape.19
  (6 shorter events, 0.1 us)
Async XLA Ops:
  0.0 8.0 %copy-start.3 = (f32[1,2,24576]{2,1,0:T(2,128)S(1)}, f32[1,2,24576]{2,1,0:T(2,128)}, u32[]{:S(2)}) copy-start(f32[1,2,24576]{2,1,0:T(2,128)} %param.14) | copy-start | bytes 589828
  0.0 8.3 %copy-start.7 = (f32[1,192]{1,0:T(1,128)S(1)}, f32[1,192]{1,0:T(1,128)}, u32[]{:S(2)}) copy-start(f32[1,192]{1,0:T(1,128)} %param.16) | copy-start | bytes 2308
  0.0 8.3 %copy-start.8 = (f32[1,192]{1,0:T(1,128)S(1)}, f32[1,192]{1,0:T(1,128)}, u32[]{:S(2)}) copy-start(f32[1,192]{1,0:T(1,128)} %param.13) | copy-start | bytes 2308
  1.7 6.7 %copy-start.4 = (bf16[1,192,384]{2,1,0:T(8,128)(2,1)S(1)}, bf16[1,192,384]{2,1,0:T(8,128)(2,1)}, u32[]{:S(2)}) copy-start(bf16[1,192,384]{2,1,0:T(8,128)(2,1)} %param.18) | copy-start | bytes 442372
  1.7 6.7 %copy-start.5 = (bf16[1,192,384]{2,1,0:T(8,128)(2,1)S(1)}, bf16[1,192,384]{2,1,0:T(8,128)(2,1)}, u32[]{:S(2)}) copy-start(bf16[1,192,384]{2,1,0:T(8,128)(2,1)} %param.17) | copy-start | bytes 442372
  1.8 6.7 %copy-start.6 = (bf16[1,192,192]{2,1,0:T(8,128)(2,1)S(1)}, bf16[1,192,192]{2,1,0:T(8,128)(2,1)}, u32[]{:S(2)}) copy-start(bf16[1,192,192]{2,1,0:T(8,128)(2,1)} %param.15) | copy-start | bytes 221188
  3.5 10.7 %all-to-all-start = ((bf16[8,2,256,24]{2,3,1,0:T(8,128)(2,1)}), bf16[8,2,256,24]{2,3,1,0:T(8,128)(2,1)S(1)}, u32[]{:S(2)}, u32[]{:S(2)}) async-start(bf16[8,2,256,24]{2,3,1,0:T(8,128)(2,1)} %pad.16), calls=%async_computation | async-start | bytes 393216 | tf_op jit(solution)/shard_map/all_to_all | solution.py:399
  14.8 1.3 copy-start
  14.8 1.3 copy-start.1
  14.8 1.3 copy-start.2

commit v3 on v2

--- a/solution.py
+++ b/solution.py
@@ -23,6 +23,12 @@
 MESH = pl.DeviceIdType.MESH
 BF = jnp.bfloat16
 F32 = jnp.float32
+
+
+def partner_offsets():
+    hops = lambda o: min(o[0], 4 - o[0]) + min(o[1], 8 - o[1])
+    offsets = [(dx, dy) for dx in range(4) for dy in range(8)]
+    return sorted(offsets, key=lambda o: (-hops(o), o[1] % 2, o[0]))
 
 
 def longitude_tables():
@@ -96,7 +102,7 @@
         latest, earlier = carry
         at = pl.ds(row, 1)
         current = lower[at, :] * (cosine * latest - upper[at, :] * earlier) + first[at, :]
-        table[at, :] = current
+        table[pl.ds(lax.rem(row, 2) * (LMAX // 2) + row // 2, 1), :] = current
         return (current, latest)
 
     zero = cosine * 0.0
@@ -111,17 +117,20 @@
 
 
 def kernel(
-    state_in, gains_in, filter_in, matrix_in, fourier, inverse_fourier, rows,
+    analysis, perturbations, gain_first, gain_second, gain_tiles, skip_in, mlp_in, mlp_out,
+    fourier, inverse_fourier, rows,
     out,
-    state, normed, skipped, send_one, send_two, recv_one, recv_two,
+    outgoing, begin, stage, state, normed, skipped, send_one, send_two, recv_one, recv_two,
     gains, filters, matrices, lower, upper, first, table, legendre, legendre_back, leaving,
     sent_one, sent_two, got_one, got_two, weight_sent, weight_got,
-    share_sent, share_got, out_sent, out_got, pace,
+    share_sent, share_got, out_sent, out_got, member_sent, member_got, pace,
 ):
     section = lax.axis_index("section")
     me = lax.axis_index("sht")
     core = lax.rem(me, 2)
     sibling = me + 1 - 2 * core
+    chip_x = me // 16
+    chip_y = lax.rem(me // 2, 8)
 
     barrier = pltpu.get_barrier_semaphore()
 
@@ -141,48 +150,77 @@
     lax.fori_loop(1, SHT, greet, 0)
     lax.fori_loop(1, SECTIONS, greet_column, 0)
 
+    deviations = perturbations[...].astype(F32)
+    average = jnp.sum(deviations, axis=0) * (1.0 / MEMBERS)
+    centre = analysis[...].astype(F32)
+    for member in range(MEMBERS):
+        outgoing[member] = (centre + deviations[member] - average).astype(BF)
+
+    gains[section] = jnp.zeros((8, PAD), F32)
+    gains[section, 0:1, 0:C] = gain_first[...]
+    gains[section, 1:2, 0:C] = gain_second[...]
+    tiles = [[gain_tiles[:, third, p, :] for third in range(3)] for p in range(2)]
+    turned = [[pltpu.roll(tile, HALF // 2, 1) for tile in row] for row in tiles]
+    left = lane_of((LMAX // 2, HALF)) < HALF // 2
+    even_rows, odd_rows = pl.ds(0, LMAX // 2), pl.ds(LMAX // 2, LMAX // 2)
+    for p in range(2):
+        at = pl.ds(p * HALF, HALF)
+        filters[section, even_rows, at] = tiles[p][0].astype(BF)
+        filters[section, odd_rows, at] = jnp.where(left, turned[p][1], turned[p][2]).astype(BF)
+    at = pl.ds(2 * HALF, HALF)
+    filters[section, even_rows, at] = jnp.where(left, tiles[0][1], turned[1][1]).astype(BF)
+    filters[section, odd_rows, at] = jnp.where(left, turned[0][2], tiles[1][2]).astype(BF)
     matrices[:, C:, :] = jnp.zeros((SECTIONS, PAD - C, 1024), BF)
-    matrices[section, 0:C, :] = matrix_in[...]
-    filters[section] = filter_in[...]
-    gains[section] = gains_in[...]
-    build_legendre(me, rows, lower, upper, first, table, legendre, legendre_back)
-    state[...] = state_in[...]
+    matrices[section, 0:C, 0:PAD] = jnp.concatenate(
+        [skip_in[...], jnp.zeros((C, PAD - C), BF)], axis=1
+    )
+    matrices[section, 0:C, PAD : PAD + HID] = mlp_in[...]
+    matrices[section, 0:C, PAD + HID :] = mlp_out[...]
 
     pl.semaphore_wait(barrier, SHT - 1 + SECTIONS - 1)
+
+    def member_copy(member):
+        return pltpu.make_async_remote_copy(
+            src_ref=outgoing.at[member], dst_ref=begin.at[section],
+            send_sem=member_sent.at[member], recv_sem=member_got,
+            device_id={"section": member + IDLE}, device_id_type=MESH,
+        )
+
+    for member in range(MEMBERS):
+
+        @pl.when(section != member + IDLE)
+        def _():
+            member_copy(member).start()
 
     filter_half = pl.ds(pl.multiple_of(core * (LMAX // 2), LMAX // 2), LMAX // 2)
     matrix_half = pl.ds(pl.multiple_of(core * (C // 2), C // 2), C // 2)
 
-    def weight_copies(target):
-        refs = [
-            (gains_in, gains.at[section]),
-            (filter_in.at[filter_half], filters.at[section, filter_half]),
-            (matrix_in.at[matrix_half], matrices.at[section, matrix_half]),
-        ]
-        return [
-            pltpu.make_async_remote_copy(
-                src_ref=source, dst_ref=target_ref, send_sem=weight_sent.at[i, target],
-                recv_sem=weight_got.at[i, section], device_id={"section": target},
-                device_id_type=MESH,
-            )
-            for i, (source, target_ref) in enumerate(refs)
-        ]
-
-    def send_weights():
-        for i in range(3):
-            for target in range(IDLE, SECTIONS):
-
-                @pl.when(section != target)
-                def _():
-                    weight_copies(target)[i].start()
+    def weight_copy(i, target):
+        ref = [
+            gains.at[section],
+            filters.at[section, filter_half],
+            matrices.at[section, matrix_half],
+        ][i]
+        return pltpu.make_async_remote_copy(
+            src_ref=ref, dst_ref=ref, send_sem=weight_sent.at[i, target],
+            recv_sem=weight_got.at[i, section], device_id={"section": target},
+            device_id_type=MESH,
+        )
+
+    def send_weights(i):
+        for target in range(IDLE, SECTIONS):
+
+            @pl.when(section != target)
+            def _():
+                weight_copy(i, target).start()
 
     def arrived(i, block):
-        refs = [
+        ref = [
             gains.at[block],
             filters.at[block, filter_half],
             matrices.at[block, matrix_half],
-        ]
-        pltpu.make_async_copy(refs[i], refs[i], weight_got.at[i, block]).wait()
+        ][i]
+        pltpu.make_async_copy(ref, ref, weight_got.at[i, block]).wait()
 
     def share(i, block):
         ref = filters.at[block, filter_half] if i == 0 else matrices.at[block, matrix_half]
@@ -191,27 +229,30 @@
             device_id={"sht": sibling}, device_id_type=MESH,
         )
 
-    @pl.when(section == 0)
+    send_weights(0)
+
+    @pl.when(section < IDLE)
     def _():
-        send_weights()
+        send_weights(1)
 
     @pl.when(section == 1)
     def _():
         pl.semaphore_wait(pace, 1)
-        send_weights()
+
+    @pl.when(section < IDLE)
+    def _():
+        send_weights(2)
 
     def exchange(send, recv, sent, got):
         recv[me] = send[me]
-
-        def one(t, carry):
-            to = lax.rem(me + t, SHT)
-            pltpu.make_async_remote_copy(
-                src_ref=send.at[to], dst_ref=recv.at[me], send_sem=sent, recv_sem=got,
-                device_id={"sht": to}, device_id_type=MESH,
-            ).start()
-            return carry
-
-        lax.fori_loop(1, SHT, one, 0)
+        for dx, dy in partner_offsets():
+            base = lax.rem(chip_x + dx, 4) * 16 + lax.rem(chip_y + dy, 8) * 2
+            for turn in (0, 1) if dx or dy else (1,):
+                to = base + lax.rem(core + turn, 2)
+                pltpu.make_async_remote_copy(
+                    src_ref=send.at[to], dst_ref=recv.at[me], send_sem=sent, recv_sem=got,
+                    device_id={"sht": to}, device_id_type=MESH,
+                ).start()
 
     def wait_all(buffer, semaphore):
         ref = buffer.at[pl.ds(0, SHT - 1)]
@@ -241,7 +282,8 @@
 
         @pl.when(section == block + 2)
         def _():
-            send_weights()
+            send_weights(1)
+            send_weights(2)
 
         @pl.when(away)
         def _():
@@ -368,6 +410,24 @@
 
     @pl.when(section >= IDLE)
     def _():
+        begin[section] = outgoing[section - IDLE]
+        build_legendre(me, rows, lower, upper, first, table, legendre, legendre_back)
+        slots = begin.at[pl.ds(0, SECTIONS - 1)]
+        pltpu.make_async_copy(slots, slots, member_got).wait()
+        for lat in range(2):
+            grid = begin[:, lat].astype(F32).reshape(C, NLON).T
+            for tile in range(2):
+                part = grid[:, :HALF]
+                if tile:
+                    part = jnp.concatenate(
+                        [grid[:, HALF:], jnp.zeros((NLON, PAD - C), F32)], axis=1
+                    )
+                stage[tile] = part
+                for odd in range(2):
+                    rows_of = pl.ds(odd * HALF, HALF)
+                    state[lat, rows_of, pl.ds(tile * HALF, HALF)] = stage[
+                        tile, pl.ds(odd, HALF, stride=2), :
+                    ].astype(BF)
         lax.fori_loop(0, SECTIONS, step, 0)
         for slot in range(2):
             for lat in range(2):
@@ -377,13 +437,14 @@
 
         @pl.when(section != target)
         def _():
-            for copy in weight_copies(target):
-                copy.wait_send()
+            for i in range(3):
+                weight_copy(i, target).wait_send()
 
     for member in range(MEMBERS):
 
         @pl.when(section != member + IDLE)
         def _():
+            member_copy(member).wait_send()
             for lat in range(2):
                 ref = out.at[member, lat]
                 pltpu.make_async_copy(ref, ref, out_got.at[member, lat]).wait()
@@ -392,32 +453,19 @@
 def per_device(
     analysis, perturbations, gain_first, spectral_gain, skip_weight, gain_second, mlp_in, mlp_out
 ):
-    wide = perturbations.astype(F32)
-    average = jnp.mean(wide, axis=0, keepdims=True)
-    members = (analysis.astype(F32)[None] + wide - average).astype(BF)
-    members = jnp.pad(members, ((IDLE, 0), (0, 0), (0, 0), (0, 0)))
-    slices = lax.all_to_all(members, "section", split_axis=0, concat_axis=0, tiled=True)
-    lats = slices.shape[1]
-    begin = slices.reshape(SECTIONS, lats, NLON // 2, 2, C // SECTIONS)
-    begin = jnp.transpose(begin, (1, 3, 2, 0, 4)).reshape(lats, NLON, C)
-    begin = jnp.pad(begin, ((0, 0), (0, 0), (0, PAD - C)))
-
-    gains = jnp.pad(
-        jnp.concatenate([gain_first, gain_second], axis=0), ((0, 6), (0, PAD - C))
-    )
-    g = spectral_gain[0].astype(BF).reshape(2, LMAX, C)
-    filters = jnp.concatenate([g[0, :, :HALF], g[1, :, :HALF], g[0, :, HALF:], g[1, :, HALF:]], axis=1)
-    matrices = jnp.concatenate(
-        [jnp.pad(skip_weight[0], ((0, 0), (0, PAD - C))), mlp_in[0], mlp_out[0]], axis=1
-    )
+    lats = analysis.shape[0]
+    tiles = spectral_gain[0].reshape(2, LMAX // 2, 3, HALF)
     forward, inverse = longitude_tables()
     vmem = pl.BlockSpec(memory_space=pltpu.VMEM)
     out = pl.pallas_call(
         kernel,
         out_shape=jax.ShapeDtypeStruct((MEMBERS, lats, NLON // 2, 2 * C), BF),
-        in_specs=[vmem] * 7,
+        in_specs=[vmem] * 11,
         out_specs=pl.BlockSpec(memory_space=pl.ANY),
         scratch_shapes=[
+            pltpu.VMEM((MEMBERS, lats, C // SECTIONS, NLON), BF),
+            pltpu.VMEM((SECTIONS, lats, C // SECTIONS, NLON), BF),
+            pltpu.VMEM((2, NLON, HALF), F32),
             pltpu.VMEM((2, NLON, PAD), BF),
             pltpu.VMEM((2, NLON, PAD), BF),
             pltpu.VMEM((2, NLON, PAD), F32),
@@ -445,12 +493,26 @@
             pltpu.SemaphoreType.DMA((2, SECTIONS)),
             pltpu.SemaphoreType.DMA((2, 2)),
             pltpu.SemaphoreType.DMA((MEMBERS, 2)),
+            pltpu.SemaphoreType.DMA((MEMBERS,)),
+            pltpu.SemaphoreType.DMA,
             pltpu.SemaphoreType.REGULAR,
         ],
         compiler_params=pltpu.CompilerParams(
             collective_id=0, has_side_effects=True, vmem_limit_bytes=40 * 1024 * 1024
         ),
-    )(begin, gains, filters, matrices, forward, inverse, latitude_rows())
+    )(
+        jnp.transpose(analysis, (0, 2, 1)),
+        jnp.transpose(perturbations, (0, 1, 3, 2)),
+        gain_first,
+        gain_second,
+        jnp.transpose(tiles, (1, 2, 0, 3)),
+        skip_weight[0],
+        mlp_in[0],
+        mlp_out[0],
+        forward,
+        inverse,
+        latitude_rows(),
+    )
     return out.reshape(1, MEMBERS, lats, NLON * C)
 
 

time: 216 us -> 205 us (0.949)
  the two profiles are of different devices: /device:TPU:496 before, /device:TPU:449 now
where the time goes in v3:
time: 205 us
  Pallas kernels  194 us (95%)
  local copies, waits for them, and re-layouts  10.9 us (5%)
    pallas_call x1, Pallas kernels, per_device(): pl.pallas_call(kernel, out_shape=jax.ShapeDtypeStruct((MEMBERS, lats, NLO...  194 us
    unnamed x22, local copies, waits for them, and re-layouts  9.14 us

profile of v3, /device:TPU:449, one launch (start us, length us, event | category | flops | bytes accessed | tf_op | source)
XLA Modules:
  0.0 204.6 jit_solution(11611268594431821749)
XLA Ops:
  0.0 0.0 copy-start
  0.0 0.9 copy-done
  0.9 0.0 copy-start.1
  0.9 0.9 copy-done.1
  1.8 0.0 copy-start.2
  1.8 0.9 copy-done.2
  2.7 0.0 copy-start.3
  2.8 0.9 copy-done.3
  3.7 0.0 copy-start.4
  3.7 0.9 copy-done.4
  4.6 0.0 copy-start.5
  4.6 0.9 copy-done.5
  5.5 0.0 copy-start.6
  5.5 0.9 copy-done.6
  6.4 0.0 copy-start.7
  6.4 0.7 copy-done.7
  7.1 0.0 copy-start.8
  7.1 0.7 copy-done.8
  7.8 0.0 copy-start.9
  7.8 0.7 copy-done.9
  8.5 0.0 copy-start.10
  8.5 0.7 copy-done.10
  9.2 193.7 %shard_map.109 = bf16[6,2,128,384]{3,2,1,0:T(8,128)(2,1)S(1)} custom-call(bf16[2,24,256]{2,1,0:T(8,128)(2,1)S(1)} %bitcast.15, bf16[6,2,24,256]{3,2,1,0:T(8,128)(2,1)S(1)} %bitcast.11, f32[1,192]{1,0:T(1,128)S(1)} %copy-done.9, f32[1,192]{1,0:T(1,128)S(1)} %copy-done.10, f32[64,3,2,128]{3,2,1,0:T(2,128)S(1)} %bitcast.10, bf16[192,192]{1,0:T(8,128)(2,1)S(1)} %bitcast.14, ...), custom_call_target="tpu_custom_call" | custom-call | tf_op jit(solution)/shard_map/pallas_call | solution.py:460
  202.8 1.7 reshape.3
Async XLA Ops:
  0.0 0.9 copy-start
  0.9 0.9 copy-start.1
  1.8 0.9 copy-start.2
  2.7 0.9 copy-start.3
  3.7 0.9 copy-start.4
  4.6 0.9 copy-start.5
  5.5 0.9 copy-start.6
  6.4 0.7 copy-start.7
  7.1 0.7 copy-start.8
  7.8 0.7 copy-start.9
  8.5 0.7 copy-start.10

commit v4 on v3

--- a/solution.py
+++ b/solution.py
@@ -17,7 +17,7 @@
 MEMBERS = 6
 SECTIONS = 8
 SHT = 64
-IDLE = 2
+HOME = (5, 6, 7, 0, 1, 2)
 PAD = 256
 HALF = 128
 MESH = pl.DeviceIdType.MESH
@@ -29,6 +29,13 @@
     hops = lambda o: min(o[0], 4 - o[0]) + min(o[1], 8 - o[1])
     offsets = [(dx, dy) for dx in range(4) for dy in range(8)]
     return sorted(offsets, key=lambda o: (-hops(o), o[1] % 2, o[0]))
+
+
+def partners(chip_x, chip_y, core):
+    for dx, dy in partner_offsets():
+        base = lax.rem(chip_x + dx, 4) * 16 + lax.rem(chip_y + dy, 8) * 2
+        for turn in (0, 1) if dx or dy else (1,):
+            yield base + lax.rem(core + turn, 2)
 
 
 def longitude_tables():
@@ -117,28 +124,48 @@
 
 
 def kernel(
-    analysis, perturbations, gain_first, gain_second, gain_tiles, skip_in, mlp_in, mlp_out,
-    fourier, inverse_fourier, rows,
+    analysis_in, perturbations_in, gain_first_in, gain_second_in, gain_tiles_in, skip_in,
+    mlp_in, mlp_out, fourier_in, inverse_fourier_in, rows_in,
     out,
-    outgoing, begin, stage, state, normed, skipped, send_one, send_two, recv_one, recv_two,
+    analysis, perturbations, gain_first, gain_second, gain_tiles, skip_own,
+    fourier, inverse_fourier, rows, loaded,
+    outgoing, begin, stage, state, normed, skipped,
+    send_one_main, send_two_main, recv_one_main, recv_two_main,
+    send_one_rest, send_two_rest, recv_one_rest, recv_two_rest,
     gains, filters, matrices, lower, upper, first, table, legendre, legendre_back, leaving,
-    sent_one, sent_two, got_one, got_two, weight_sent, weight_got,
+    sent, got, weight_sent, weight_got, pass_sent, pass_got,
     share_sent, share_got, out_sent, out_got, member_sent, member_got, pace,
 ):
     section = lax.axis_index("section")
     me = lax.axis_index("sht")
     core = lax.rem(me, 2)
     sibling = me + 1 - 2 * core
+    own = lax.rem(section + 3, SECTIONS)
+    holds = own < MEMBERS
     chip_x = me // 16
     chip_y = lax.rem(me // 2, 8)
 
+    loads = [
+        pltpu.make_async_copy(source, target, loaded.at[i])
+        for i, (source, target) in enumerate(
+            [
+                (perturbations_in, perturbations),
+                (analysis_in, analysis),
+                (gain_first_in, gain_first),
+                (gain_second_in, gain_second),
+                (gain_tiles_in, gain_tiles),
+                (skip_in, skip_own),
+                (mlp_in, matrices.at[section, pl.ds(0, C), pl.ds(PAD, HID)]),
+                (mlp_out, matrices.at[section, pl.ds(0, C), pl.ds(PAD + HID, HID)]),
+                (rows_in, rows),
+                (fourier_in, fourier),
+                (inverse_fourier_in, inverse_fourier),
+            ]
+        )
+    ]
+    for load in loads:
+        load.start()
     barrier = pltpu.get_barrier_semaphore()
-
-    def greet(t, carry):
-        pl.semaphore_signal(
-            barrier, inc=1, device_id={"sht": lax.rem(me + t, SHT)}, device_id_type=MESH
-        )
-        return carry
 
     def greet_column(t, carry):
         pl.semaphore_signal(
@@ -147,15 +174,20 @@
         )
         return carry
 
-    lax.fori_loop(1, SHT, greet, 0)
+    for to in partners(chip_x, chip_y, core):
+        pl.semaphore_signal(barrier, inc=1, device_id={"sht": to}, device_id_type=MESH)
     lax.fori_loop(1, SECTIONS, greet_column, 0)
 
+    loads[0].wait()
+    loads[1].wait()
     deviations = perturbations[...].astype(F32)
     average = jnp.sum(deviations, axis=0) * (1.0 / MEMBERS)
     centre = analysis[...].astype(F32)
     for member in range(MEMBERS):
         outgoing[member] = (centre + deviations[member] - average).astype(BF)
 
+    for load in loads[2:8]:
+        load.wait()
     gains[section] = jnp.zeros((8, PAD), F32)
     gains[section, 0:1, 0:C] = gain_first[...]
     gains[section, 1:2, 0:C] = gain_second[...]
@@ -172,10 +204,10 @@
     filters[section, odd_rows, at] = jnp.where(left, turned[0][2], tiles[1][2]).astype(BF)
     matrices[:, C:, :] = jnp.zeros((SECTIONS, PAD - C, 1024), BF)
     matrices[section, 0:C, 0:PAD] = jnp.concatenate(
-        [skip_in[...], jnp.zeros((C, PAD - C), BF)], axis=1
+        [skip_own[...], jnp.zeros((C, PAD - C), BF)], axis=1
     )
-    matrices[section, 0:C, PAD : PAD + HID] = mlp_in[...]
-    matrices[section, 0:C, PAD + HID :] = mlp_out[...]
+    for load in loads[8:]:
+        load.wait()
 
     pl.semaphore_wait(barrier, SHT - 1 + SECTIONS - 1)
 
@@ -183,24 +215,29 @@
         return pltpu.make_async_remote_copy(
             src_ref=outgoing.at[member], dst_ref=begin.at[section],
             send_sem=member_sent.at[member], recv_sem=member_got,
-            device_id={"section": member + IDLE}, device_id_type=MESH,
+            device_id={"section": HOME[member]}, device_id_type=MESH,
         )
 
     for member in range(MEMBERS):
 
-        @pl.when(section != member + IDLE)
+        @pl.when(section != HOME[member])
         def _():
             member_copy(member).start()
 
     filter_half = pl.ds(pl.multiple_of(core * (LMAX // 2), LMAX // 2), LMAX // 2)
-    matrix_half = pl.ds(pl.multiple_of(core * (C // 2), C // 2), C // 2)
+    matrix_half = pl.ds(pl.multiple_of(core * 512, 512), 512)
+    filter_piece = pl.ds(pl.multiple_of(core * 64 + chip_x * 16, 16), 16)
+    matrix_piece = pl.ds(pl.multiple_of(core * 512 + chip_x * HALF, HALF), HALF)
+
+    def part_of(i, block, piece):
+        if i == 0:
+            return gains.at[block]
+        if i == 1:
+            return filters.at[block, filter_piece if piece else filter_half]
+        return matrices.at[block, pl.ds(0, C), matrix_piece if piece else matrix_half]
 
     def weight_copy(i, target):
-        ref = [
-            gains.at[section],
-            filters.at[section, filter_half],
-            matrices.at[section, matrix_half],
-        ][i]
+        ref = part_of(i, section, True)
         return pltpu.make_async_remote_copy(
             src_ref=ref, dst_ref=ref, send_sem=weight_sent.at[i, target],
             recv_sem=weight_got.at[i, section], device_id={"section": target},
@@ -208,51 +245,63 @@
         )
 
     def send_weights(i):
-        for target in range(IDLE, SECTIONS):
+        for target in HOME:
 
             @pl.when(section != target)
             def _():
                 weight_copy(i, target).start()
 
     def arrived(i, block):
-        ref = [
-            gains.at[block],
-            filters.at[block, filter_half],
-            matrices.at[block, matrix_half],
-        ][i]
+        ref = part_of(i, block, True)
         pltpu.make_async_copy(ref, ref, weight_got.at[i, block]).wait()
 
     def share(i, block):
-        ref = filters.at[block, filter_half] if i == 0 else matrices.at[block, matrix_half]
+        ref = part_of(i, block, False)
         return pltpu.make_async_remote_copy(
             src_ref=ref, dst_ref=ref, send_sem=share_sent.at[i], recv_sem=share_got.at[i, block],
             device_id={"sht": sibling}, device_id_type=MESH,
         )
 
+    def pass_along(i, block, step):
+        ref = part_of(i, block, True)
+        to = lax.rem(chip_x + step, 4) * 16 + lax.rem(me, 16)
+        return pltpu.make_async_remote_copy(
+            src_ref=ref, dst_ref=ref, send_sem=pass_sent.at[i, step],
+            recv_sem=pass_got.at[i, block], device_id={"sht": to}, device_id_type=MESH,
+        )
+
+    def hand_out(block):
+        for i in (1, 2):
+            arrived(i, block)
+            for step in range(1, 4):
+                pass_along(i, block, step).start()
+
+    def collect(i, block):
+        ref = filters.at[0, pl.ds(0, 48)] if i == 1 else matrices.at[0, pl.ds(0, C), pl.ds(0, 384)]
+        pltpu.make_async_copy(ref, ref, pass_got.at[i, block]).wait()
+        for step in range(1, 4):
+            pass_along(i, block, step).wait_send()
+
     send_weights(0)
 
-    @pl.when(section < IDLE)
+    @pl.when(section == 0)
     def _():
         send_weights(1)
-
-    @pl.when(section == 1)
+        send_weights(2)
+
+    @pl.when(jnp.logical_not(holds))
     def _():
         pl.semaphore_wait(pace, 1)
-
-    @pl.when(section < IDLE)
-    def _():
+        send_weights(1)
         send_weights(2)
 
     def exchange(send, recv, sent, got):
         recv[me] = send[me]
-        for dx, dy in partner_offsets():
-            base = lax.rem(chip_x + dx, 4) * 16 + lax.rem(chip_y + dy, 8) * 2
-            for turn in (0, 1) if dx or dy else (1,):
-                to = base + lax.rem(core + turn, 2)
-                pltpu.make_async_remote_copy(
-                    src_ref=send.at[to], dst_ref=recv.at[me], send_sem=sent, recv_sem=got,
-                    device_id={"sht": to}, device_id_type=MESH,
-                ).start()
+        for to in partners(chip_x, chip_y, core):
+            pltpu.make_async_remote_copy(
+                src_ref=send.at[to], dst_ref=recv.at[me], send_sem=sent, recv_sem=got,
+                device_id={"sht": to}, device_id_type=MESH,
+            ).start()
 
     def wait_all(buffer, semaphore):
         ref = buffer.at[pl.ds(0, SHT - 1)]
@@ -279,11 +328,6 @@
 
     def step(block, carry):
         away = section != block
-
-        @pl.when(section == block + 2)
-        def _():
-            send_weights(1)
-            send_weights(2)
 
         @pl.when(away)
         def _():
@@ -296,23 +340,24 @@
             turned = pltpu.roll(wide[:, HALF:], HALF // 2, 1).astype(BF)
             real = dot(fourier[0], narrow)
             imag = dot(fourier[1], jnp.concatenate([narrow[:, :HALF], turned], axis=1))
-            spectrum = jnp.concatenate(
-                [real[:, :HALF], imag[:, :HALF], real[:, HALF:] + imag[:, HALF:]], axis=1
-            ).astype(BF)
-            send_one[:, 2 * lat : 2 * lat + 2, :] = spectrum.reshape(SHT, 2, 2 * C)
-        exchange(send_one, recv_one, sent_one, got_one)
+            at = pl.ds(2 * lat, 2)
+            main = jnp.concatenate([real[:, :HALF], imag[:, :HALF]], axis=1).astype(BF)
+            rest = (real[:, HALF:] + imag[:, HALF:]).astype(BF)
+            send_one_main[:, at, :] = main.reshape(SHT, 2, 2 * HALF)
+            send_one_rest[:, at, :] = rest.reshape(SHT, 2, HALF)
+        exchange(send_one_main, recv_one_main, sent.at[0], got.at[0])
+        exchange(send_one_rest, recv_one_rest, sent.at[1], got.at[1])
+
+        @pl.when(jnp.logical_and(away, block == 0))
+        def _():
+            hand_out(0)
 
         @pl.when(away)
         def _():
-            arrived(1, block)
-            share(0, block).start()
-
-        wait_all(recv_one, got_one)
-        coeffs = dot(legendre[...], recv_one[...].reshape(2 * NLAT, 2 * C))
-
-        @pl.when(away)
-        def _():
-            share(0, block).wait()
+            collect(1, block)
+            copy = share(1, block)
+            copy.start()
+            copy.wait()
 
         gain = filters[block].astype(F32)
         gain_real, gain_imag = gain[:, :HALF], gain[:, HALF : 2 * HALF]
@@ -320,38 +365,60 @@
         gain_turned = pltpu.roll(gain_rest, HALF // 2, 1)
         gain_straight = jnp.where(low, gain_rest, gain_turned)
         gain_cross = jnp.where(low, -gain_turned, gain_rest)
+
+        wait_all(recv_one_main, got.at[0])
+        coeffs = dot(legendre[...], recv_one_main[...].reshape(2 * NLAT, 2 * HALF))
         parts = []
         for order in range(2):
             part = coeffs[order * LMAX : (order + 1) * LMAX]
-            real, imag, rest = part[:, :HALF], part[:, HALF : 2 * HALF], part[:, 2 * HALF :]
+            real, imag = part[:, :HALF], part[:, HALF:]
             parts.append(
                 jnp.concatenate(
-                    [
-                        real * gain_real - imag * gain_imag,
-                        real * gain_imag + imag * gain_real,
-                        rest * gain_straight + pltpu.roll(rest, HALF // 2, 1) * gain_cross,
-                    ],
+                    [real * gain_real - imag * gain_imag, real * gain_imag + imag * gain_real],
                     axis=1,
                 )
             )
         filtered = jnp.concatenate(parts, axis=0).astype(BF)
         returned = dot(legendre_back[...], filtered).astype(BF)
-
-        wait_all(send_one, sent_one)
-
-        send_two[...] = returned.reshape(SHT, 4, 2 * C)
-        exchange(send_two, recv_two, sent_two, got_two)
+        send_two_main[...] = returned.reshape(SHT, 4, 2 * HALF)
+        exchange(send_two_main, recv_two_main, sent.at[2], got.at[2])
+
+        wait_all(recv_one_rest, got.at[1])
+        coeffs = dot(legendre[...], recv_one_rest[...].reshape(2 * NLAT, HALF))
+        parts = []
+        for order in range(2):
+            rest = coeffs[order * LMAX : (order + 1) * LMAX]
+            parts.append(rest * gain_straight + pltpu.roll(rest, HALF // 2, 1) * gain_cross)
+        filtered = jnp.concatenate(parts, axis=0).astype(BF)
+        returned = dot(legendre_back[...], filtered).astype(BF)
+        send_two_rest[...] = returned.reshape(SHT, 4, HALF)
+        exchange(send_two_rest, recv_two_rest, sent.at[3], got.at[3])
 
         @pl.when(away)
         def _():
-            arrived(2, block)
-            copy = share(1, block)
+            collect(2, block)
+            copy = share(2, block)
             copy.start()
             copy.wait()
 
-        @pl.when(jnp.logical_and(block == 0, section == 4))
-        def _():
-            pl.semaphore_signal(pace, inc=1, device_id={"section": 1}, device_id_type=MESH)
+        following = jnp.minimum(block + 1, SECTIONS - 1)
+
+        @pl.when(jnp.logical_and(section != following, block < SECTIONS - 1))
+        def _():
+            hand_out(following)
+
+        @pl.when(jnp.logical_and(section == block + 2, holds))
+        def _():
+            send_weights(1)
+            send_weights(2)
+
+        for turn in (1, 2):
+
+            @pl.when(jnp.logical_and(block == turn, section == 2))
+            def _():
+                pl.semaphore_signal(
+                    pace, inc=1, device_id={"section": turn + 2}, device_id_type=MESH
+                )
 
         skip = matrices[block, :, 0:PAD]
         into = matrices[block, :, PAD : PAD + HID]
@@ -359,17 +426,21 @@
         for lat in range(2):
             skipped[lat] = dot(normed[lat], skip)
 
-        wait_all(recv_two, got_two)
+        wait_all(send_one_main, sent.at[0])
+        wait_all(send_one_rest, sent.at[1])
+        wait_all(recv_two_main, got.at[2])
+        wait_all(recv_two_rest, got.at[3])
         slot = lax.rem(block, 2)
         for lat in range(2):
-            waves = recv_two[:, 2 * lat : 2 * lat + 2, :].reshape(MMAX, 2 * C)
-            rest = waves[:, 2 * HALF :].astype(F32)
+            at = pl.ds(2 * lat, 2)
+            waves = recv_two_main[:, at, :].reshape(MMAX, 2 * HALF)
+            rest = recv_two_rest[:, at, :].reshape(MMAX, HALF).astype(F32)
             top = jnp.where(low, rest, 0.0).astype(BF)
             bottom = jnp.where(low, pltpu.roll(rest, HALF // 2, 1), 0.0).astype(BF)
             stacked = jnp.concatenate(
                 [
                     jnp.concatenate([waves[:, :HALF], top], axis=1),
-                    jnp.concatenate([waves[:, HALF : 2 * HALF], bottom], axis=1),
+                    jnp.concatenate([waves[:, HALF:], bottom], axis=1),
                 ],
                 axis=0,
             )
@@ -399,21 +470,28 @@
 
             @pl.when(away)
             def _():
-                out_copy(lat, slot, section - IDLE, block).start()
+                out_copy(lat, slot, own, block).start()
 
             @pl.when(jnp.logical_not(away))
             def _():
-                own_copy(lat, slot, section - IDLE).start()
-
-        wait_all(send_two, sent_two)
+                own_copy(lat, slot, own).start()
+
+        wait_all(send_two_main, sent.at[2])
+        wait_all(send_two_rest, sent.at[3])
         return carry
 
-    @pl.when(section >= IDLE)
+    @pl.when(holds)
     def _():
-        begin[section] = outgoing[section - IDLE]
+        begin[section] = outgoing[own]
         build_legendre(me, rows, lower, upper, first, table, legendre, legendre_back)
         slots = begin.at[pl.ds(0, SECTIONS - 1)]
         pltpu.make_async_copy(slots, slots, member_got).wait()
+
+        @pl.when(section == 1)
+        def _():
+            send_weights(1)
+            send_weights(2)
+
         for lat in range(2):
             grid = begin[:, lat].astype(F32).reshape(C, NLON).T
             for tile in range(2):
@@ -433,7 +511,7 @@
             for lat in range(2):
                 wait_left(lat, slot)
 
-    for target in range(IDLE, SECTIONS):
+    for target in HOME:
 
         @pl.when(section != target)
         def _():
@@ -442,7 +520,7 @@
 
     for member in range(MEMBERS):
 
-        @pl.when(section != member + IDLE)
+        @pl.when(section != HOME[member])
         def _():
             member_copy(member).wait_send()
             for lat in range(2):
@@ -456,23 +534,31 @@
     lats = analysis.shape[0]
     tiles = spectral_gain[0].reshape(2, LMAX // 2, 3, HALF)
     forward, inverse = longitude_tables()
-    vmem = pl.BlockSpec(memory_space=pltpu.VMEM)
+    hbm = pl.BlockSpec(memory_space=pltpu.HBM)
     out = pl.pallas_call(
         kernel,
         out_shape=jax.ShapeDtypeStruct((MEMBERS, lats, NLON // 2, 2 * C), BF),
-        in_specs=[vmem] * 11,
-        out_specs=pl.BlockSpec(memory_space=pl.ANY),
+        in_specs=[hbm] * 11,
+        out_specs=hbm,
         scratch_shapes=[
+            pltpu.VMEM((lats, C // SECTIONS, NLON), BF),
+            pltpu.VMEM((MEMBERS, lats, C // SECTIONS, NLON), BF),
+            pltpu.VMEM((1, C), F32),
+            pltpu.VMEM((1, C), F32),
+            pltpu.VMEM((LMAX // 2, 3, 2, HALF), F32),
+            pltpu.VMEM((C, C), BF),
+            pltpu.VMEM((2, MMAX, NLON), BF),
+            pltpu.VMEM((NLON, 2 * MMAX), BF),
+            pltpu.VMEM((8, 2 * NLAT), F32),
+            pltpu.SemaphoreType.DMA((11,)),
             pltpu.VMEM((MEMBERS, lats, C // SECTIONS, NLON), BF),
             pltpu.VMEM((SECTIONS, lats, C // SECTIONS, NLON), BF),
             pltpu.VMEM((2, NLON, HALF), F32),
             pltpu.VMEM((2, NLON, PAD), BF),
             pltpu.VMEM((2, NLON, PAD), BF),
             pltpu.VMEM((2, NLON, PAD), F32),
-            pltpu.VMEM((SHT, 4, 2 * C), BF),
-            pltpu.VMEM((SHT, 4, 2 * C), BF),
-            pltpu.VMEM((SHT, 4, 2 * C), BF),
-            pltpu.VMEM((SHT, 4, 2 * C), BF),
+            *[pltpu.VMEM((SHT, 4, 2 * HALF), BF)] * 4,
+            *[pltpu.VMEM((SHT, 4, HALF), BF)] * 4,
             pltpu.VMEM((SECTIONS, 8, PAD), F32),
             pltpu.VMEM((SECTIONS, LMAX, 2 * C), BF),
             pltpu.VMEM((SECTIONS, PAD, 1024), BF),
@@ -483,14 +569,14 @@
             pltpu.VMEM((2 * LMAX, 2 * NLAT), BF),
             pltpu.VMEM((2 * NLAT, 2 * LMAX), BF),
             pltpu.VMEM((2, 2, NLON // 2, 2 * C), BF),
-            pltpu.SemaphoreType.DMA,
-            pltpu.SemaphoreType.DMA,
-            pltpu.SemaphoreType.DMA,
-            pltpu.SemaphoreType.DMA,
+            pltpu.SemaphoreType.DMA((4,)),
+            pltpu.SemaphoreType.DMA((4,)),
             pltpu.SemaphoreType.DMA((3, SECTIONS)),
             pltpu.SemaphoreType.DMA((3, SECTIONS)),
-            pltpu.SemaphoreType.DMA((2,)),
-            pltpu.SemaphoreType.DMA((2, SECTIONS)),
+            pltpu.SemaphoreType.DMA((3, 4)),
+            pltpu.SemaphoreType.DMA((3, SECTIONS)),
+            pltpu.SemaphoreType.DMA((3,)),
+            pltpu.SemaphoreType.DMA((3, SECTIONS)),
             pltpu.SemaphoreType.DMA((2, 2)),
             pltpu.SemaphoreType.DMA((MEMBERS, 2)),
             pltpu.SemaphoreType.DMA((MEMBERS,)),
@@ -498,7 +584,7 @@
             pltpu.SemaphoreType.REGULAR,
         ],
         compiler_params=pltpu.CompilerParams(
-            collective_id=0, has_side_effects=True, vmem_limit_bytes=40 * 1024 * 1024
+            collective_id=0, has_side_effects=True, vmem_limit_bytes=67_000_000
         ),
     )(
         jnp.transpose(analysis, (0, 2, 1)),

time: 205 us -> 188 us (0.917)
  the two profiles are of different devices: /device:TPU:449 before, /device:TPU:1 now
where the time goes in v4:
time: 188 us
  Pallas kernels  185 us (98%)
  local copies, waits for them, and re-layouts  3.22 us (2%)
    pallas_call x1, Pallas kernels, per_device(): pl.pallas_call(kernel, out_shape=jax.ShapeDtypeStruct((MEMBERS, lats, NLO...  185 us

profile of v4, /device:TPU:1, one launch (start us, length us, event | category | flops | bytes accessed | tf_op | source)
XLA Modules:
  0.0 188.1 jit_solution(18160132097310180630)
XLA Ops:
  0.0 184.9 %shard_map.109 = bf16[6,2,128,384]{3,2,1,0:T(8,128)(2,1)} custom-call(bf16[2,24,256]{2,1,0:T(8,128)(2,1)} %bitcast.15, bf16[6,2,24,256]{3,2,1,0:T(8,128)(2,1)} %bitcast.11, f32[1,192]{1,0:T(1,128)} %gain_first_in.1, f32[1,192]{1,0:T(1,128)} %gain_second_in.1, f32[64,3,2,128]{3,2,1,0:T(2,128)} %bitcast.10, bf16[192,192]{1,0:T(8,128)(2,1)} %bitcast.14, ...), custom_call_target="tpu_custom_call" | custom-call | tf_op jit(solution)/shard_map/pallas_call | solution.py:538
  184.9 3.2 %reshape.3 = bf16[1,6,2,49152]{3,2,1,0:T(2,128)(2,1)} reshape(bf16[6,2,128,384]{3,2,1,0:T(8,128)(2,1)} %shard_map.109) | data formatting | bytes 2359296 | tf_op jit(solution)/shard_map/reshape | solution.py:602

commit v5 on v4

--- a/solution.py
+++ b/solution.py
@@ -54,7 +54,8 @@
 
 def latitude_rows():
     lane = np.arange(2 * NLAT)
-    colatitude = (math.pi * (lane // 2 + 0.5) / NLAT).astype(np.float32)
+    latitude = 2 * (lane % NLAT // 2) + lane // NLAT
+    colatitude = (math.pi * (latitude + 0.5) / NLAT).astype(np.float32)
     sine = np.sin(colatitude)
     rows = np.zeros((8, 2 * NLAT), np.float32)
     rows[0] = np.cos(colatitude)
@@ -130,8 +131,7 @@
     analysis, perturbations, gain_first, gain_second, gain_tiles, skip_own,
     fourier, inverse_fourier, rows, loaded,
     outgoing, begin, stage, state, normed, skipped,
-    send_one_main, send_two_main, recv_one_main, recv_two_main,
-    send_one_rest, send_two_rest, recv_one_rest, recv_two_rest,
+    send_one, send_two, recv_one, recv_two,
     gains, filters, matrices, lower, upper, first, table, legendre, legendre_back, leaving,
     sent, got, weight_sent, weight_got, pass_sent, pass_got,
     share_sent, share_got, out_sent, out_got, member_sent, member_got, pace,
@@ -215,12 +215,13 @@
         return pltpu.make_async_remote_copy(
             src_ref=outgoing.at[member], dst_ref=begin.at[section],
             send_sem=member_sent.at[member], recv_sem=member_got,
-            device_id={"section": HOME[member]}, device_id_type=MESH,
-        )
-
-    for member in range(MEMBERS):
-
-        @pl.when(section != HOME[member])
+            device_id={"section": lax.rem(member + 5, SECTIONS)}, device_id_type=MESH,
+        )
+
+    for turn in (4, 3, 5, 2, 6, 1, 7):
+        member = lax.rem(own + turn, SECTIONS)
+
+        @pl.when(member < MEMBERS)
         def _():
             member_copy(member).start()
 
@@ -326,27 +327,21 @@
     low = lane_of((HALF, HALF)) < HALF // 2
     low_all = lane_of((NLON, HALF)) < HALF // 2
 
+    def begin_block(lat, block):
+        wide = layer_norm(state[lat].astype(F32), gains[block, 0:1, :])
+        narrow = wide.astype(BF)
+        normed[lat] = narrow
+        turned = pltpu.roll(wide[:, HALF:], HALF // 2, 1).astype(BF)
+        real = dot(fourier[0], narrow)
+        imag = dot(fourier[1], jnp.concatenate([narrow[:, :HALF], turned], axis=1))
+        spectrum = jnp.concatenate(
+            [real[:, :HALF], imag[:, :HALF], real[:, HALF:] + imag[:, HALF:]], axis=1
+        ).astype(BF)
+        send_one[lat] = spectrum.reshape(SHT, 2, 2 * C)
+        exchange(send_one.at[lat], recv_one.at[lat], sent.at[lat], got.at[lat])
+
     def step(block, carry):
         away = section != block
-
-        @pl.when(away)
-        def _():
-            arrived(0, block)
-
-        for lat in range(2):
-            wide = layer_norm(state[lat].astype(F32), gains[block, 0:1, :])
-            narrow = wide.astype(BF)
-            normed[lat] = narrow
-            turned = pltpu.roll(wide[:, HALF:], HALF // 2, 1).astype(BF)
-            real = dot(fourier[0], narrow)
-            imag = dot(fourier[1], jnp.concatenate([narrow[:, :HALF], turned], axis=1))
-            at = pl.ds(2 * lat, 2)
-            main = jnp.concatenate([real[:, :HALF], imag[:, :HALF]], axis=1).astype(BF)
-            rest = (real[:, HALF:] + imag[:, HALF:]).astype(BF)
-            send_one_main[:, at, :] = main.reshape(SHT, 2, 2 * HALF)
-            send_one_rest[:, at, :] = rest.reshape(SHT, 2, HALF)
-        exchange(send_one_main, recv_one_main, sent.at[0], got.at[0])
-        exchange(send_one_rest, recv_one_rest, sent.at[1], got.at[1])
 
         @pl.when(jnp.logical_and(away, block == 0))
         def _():
@@ -366,33 +361,29 @@
         gain_straight = jnp.where(low, gain_rest, gain_turned)
         gain_cross = jnp.where(low, -gain_turned, gain_rest)
 
-        wait_all(recv_one_main, got.at[0])
-        coeffs = dot(legendre[...], recv_one_main[...].reshape(2 * NLAT, 2 * HALF))
+        wait_all(recv_one.at[0], got.at[0])
+        coeffs = dot(legendre[:, :NLAT], recv_one[0].reshape(NLAT, 2 * C))
+        wait_all(recv_one.at[1], got.at[1])
+        coeffs = coeffs + dot(legendre[:, NLAT:], recv_one[1].reshape(NLAT, 2 * C))
         parts = []
         for order in range(2):
             part = coeffs[order * LMAX : (order + 1) * LMAX]
-            real, imag = part[:, :HALF], part[:, HALF:]
+            real, imag, rest = part[:, :HALF], part[:, HALF : 2 * HALF], part[:, 2 * HALF :]
             parts.append(
                 jnp.concatenate(
-                    [real * gain_real - imag * gain_imag, real * gain_imag + imag * gain_real],
+                    [
+                        real * gain_real - imag * gain_imag,
+                        real * gain_imag + imag * gain_real,
+                        rest * gain_straight + pltpu.roll(rest, HALF // 2, 1) * gain_cross,
+                    ],
                     axis=1,
                 )
             )
         filtered = jnp.concatenate(parts, axis=0).astype(BF)
-        returned = dot(legendre_back[...], filtered).astype(BF)
-        send_two_main[...] = returned.reshape(SHT, 4, 2 * HALF)
-        exchange(send_two_main, recv_two_main, sent.at[2], got.at[2])
-
-        wait_all(recv_one_rest, got.at[1])
-        coeffs = dot(legendre[...], recv_one_rest[...].reshape(2 * NLAT, HALF))
-        parts = []
-        for order in range(2):
-            rest = coeffs[order * LMAX : (order + 1) * LMAX]
-            parts.append(rest * gain_straight + pltpu.roll(rest, HALF // 2, 1) * gain_cross)
-        filtered = jnp.concatenate(parts, axis=0).astype(BF)
-        returned = dot(legendre_back[...], filtered).astype(BF)
-        send_two_rest[...] = returned.reshape(SHT, 4, HALF)
-        exchange(send_two_rest, recv_two_rest, sent.at[3], got.at[3])
+        for lat in range(2):
+            returned = dot(legendre_back[lat * NLAT : (lat + 1) * NLAT, :], filtered).astype(BF)
+            send_two[lat] = returned.reshape(SHT, 2, 2 * C)
+            exchange(send_two.at[lat], recv_two.at[lat], sent.at[2 + lat], got.at[2 + lat])
 
         @pl.when(away)
         def _():
@@ -405,6 +396,7 @@
 
         @pl.when(jnp.logical_and(section != following, block < SECTIONS - 1))
         def _():
+            arrived(0, following)
             hand_out(following)
 
         @pl.when(jnp.logical_and(section == block + 2, holds))
@@ -426,21 +418,19 @@
         for lat in range(2):
             skipped[lat] = dot(normed[lat], skip)
 
-        wait_all(send_one_main, sent.at[0])
-        wait_all(send_one_rest, sent.at[1])
-        wait_all(recv_two_main, got.at[2])
-        wait_all(recv_two_rest, got.at[3])
+        for lat in range(2):
+            wait_all(send_one.at[lat], sent.at[lat])
         slot = lax.rem(block, 2)
         for lat in range(2):
-            at = pl.ds(2 * lat, 2)
-            waves = recv_two_main[:, at, :].reshape(MMAX, 2 * HALF)
-            rest = recv_two_rest[:, at, :].reshape(MMAX, HALF).astype(F32)
+            wait_all(recv_two.at[lat], got.at[2 + lat])
+            waves = recv_two[lat].reshape(MMAX, 2 * C)
+            rest = waves[:, 2 * HALF :].astype(F32)
             top = jnp.where(low, rest, 0.0).astype(BF)
             bottom = jnp.where(low, pltpu.roll(rest, HALF // 2, 1), 0.0).astype(BF)
             stacked = jnp.concatenate(
                 [
                     jnp.concatenate([waves[:, :HALF], top], axis=1),
-                    jnp.concatenate([waves[:, HALF:], bottom], axis=1),
+                    jnp.concatenate([waves[:, HALF : 2 * HALF], bottom], axis=1),
                 ],
                 axis=0,
             )
@@ -453,6 +443,10 @@
             result = state[lat].astype(F32) + update
             state[lat] = result.astype(BF)
 
+            @pl.when(block < SECTIONS - 1)
+            def _():
+                begin_block(lat, following)
+
             @pl.when(block >= 2)
             def _():
                 wait_left(lat, slot)
@@ -476,8 +470,8 @@
             def _():
                 own_copy(lat, slot, own).start()
 
-        wait_all(send_two_main, sent.at[2])
-        wait_all(send_two_rest, sent.at[3])
+        for lat in range(2):
+            wait_all(send_two.at[lat], sent.at[2 + lat])
         return carry
 
     @pl.when(holds)
@@ -506,6 +500,13 @@
                     state[lat, rows_of, pl.ds(tile * HALF, HALF)] = stage[
                         tile, pl.ds(odd, HALF, stride=2), :
                     ].astype(BF)
+
+        @pl.when(section != 0)
+        def _():
+            arrived(0, 0)
+
+        for lat in range(2):
+            begin_block(lat, 0)
         lax.fori_loop(0, SECTIONS, step, 0)
         for slot in range(2):
             for lat in range(2):
@@ -557,8 +558,7 @@
             pltpu.VMEM((2, NLON, PAD), BF),
             pltpu.VMEM((2, NLON, PAD), BF),
             pltpu.VMEM((2, NLON, PAD), F32),
-            *[pltpu.VMEM((SHT, 4, 2 * HALF), BF)] * 4,
-            *[pltpu.VMEM((SHT, 4, HALF), BF)] * 4,
+            *[pltpu.VMEM((lats, SHT, 2, 2 * C), BF)] * 4,
             pltpu.VMEM((SECTIONS, 8, PAD), F32),
             pltpu.VMEM((SECTIONS, LMAX, 2 * C), BF),
             pltpu.VMEM((SECTIONS, PAD, 1024), BF),

time: 188 us -> 174 us (0.926)
  Pallas kernels: 185 us -> 171 us
    pallas_call x1, Pallas kernels: 185 us -> 171 us  [per_device(): pl.pallas_call(kernel, out_shape=jax.ShapeDtypeStruct((MEMBERS, lats, NLO...]
where the time goes in v5:
time: 174 us
  Pallas kernels  171 us (98%)
  local copies, waits for them, and re-layouts  3.22 us (2%)
    pallas_call x1, Pallas kernels, per_device(): pl.pallas_call(kernel, out_shape=jax.ShapeDtypeStruct((MEMBERS, lats, NLO...  171 us

profile of v5, /device:TPU:1, one launch (start us, length us, event | category | flops | bytes accessed | tf_op | source)
XLA Modules:
  0.0 173.9 jit_solution(4717845191154973106)
XLA Ops:
  0.0 170.6 %shard_map.109 = bf16[6,2,128,384]{3,2,1,0:T(8,128)(2,1)} custom-call(bf16[2,24,256]{2,1,0:T(8,128)(2,1)} %bitcast.15, bf16[6,2,24,256]{3,2,1,0:T(8,128)(2,1)} %bitcast.11, f32[1,192]{1,0:T(1,128)} %gain_first_in.1, f32[1,192]{1,0:T(1,128)} %gain_second_in.1, f32[64,3,2,128]{3,2,1,0:T(2,128)} %bitcast.10, bf16[192,192]{1,0:T(8,128)(2,1)} %bitcast.14, ...), custom_call_target="tpu_custom_call" | custom-call | tf_op jit(solution)/shard_map/pallas_call | solution.py:539
  170.6 3.2 %reshape.3 = bf16[1,6,2,49152]{3,2,1,0:T(2,128)(2,1)} reshape(bf16[6,2,128,384]{3,2,1,0:T(8,128)(2,1)} %shard_map.109) | data formatting | bytes 2359296 | tf_op jit(solution)/shard_map/reshape | solution.py:602

commit v6 on v5

--- a/solution.py
+++ b/solution.py
@@ -19,6 +19,7 @@
 SHT = 64
 HOME = (5, 6, 7, 0, 1, 2)
 PAD = 256
+FAR = 32
 HALF = 128
 MESH = pl.DeviceIdType.MESH
 BF = jnp.bfloat16
@@ -129,7 +130,7 @@
     mlp_in, mlp_out, fourier_in, inverse_fourier_in, rows_in,
     out,
     analysis, perturbations, gain_first, gain_second, gain_tiles, skip_own,
-    fourier, inverse_fourier, rows, loaded,
+    fourier, inverse_fourier, rows, loaded, relay, relay_sent, relay_got,
     outgoing, begin, stage, state, normed, skipped,
     send_one, send_two, recv_one, recv_two,
     gains, filters, matrices, lower, upper, first, table, legendre, legendre_back, leaving,
@@ -296,9 +297,10 @@
         send_weights(1)
         send_weights(2)
 
-    def exchange(send, recv, sent, got):
-        recv[me] = send[me]
-        for to in partners(chip_x, chip_y, core):
+    def exchange(send, recv, sent, got, first=0, last=SHT - 1):
+        if first == 0:
+            recv[me] = send[me]
+        for to in list(partners(chip_x, chip_y, core))[first:last]:
             pltpu.make_async_remote_copy(
                 src_ref=send.at[to], dst_ref=recv.at[me], send_sem=sent, recv_sem=got,
                 device_id={"sht": to}, device_id_type=MESH,
@@ -313,6 +315,18 @@
             src_ref=leaving.at[slot, lat], dst_ref=out.at[member, lat],
             send_sem=out_sent.at[slot, lat], recv_sem=out_got.at[member, lat],
             device_id={"section": block}, device_id_type=MESH,
+        )
+
+    def to_relay():
+        return pltpu.make_async_remote_copy(
+            src_ref=leaving.at[1, 0], dst_ref=relay, send_sem=out_sent.at[1, 0],
+            recv_sem=relay_got, device_id={"section": 4}, device_id_type=MESH,
+        )
+
+    def from_relay():
+        return pltpu.make_async_remote_copy(
+            src_ref=relay, dst_ref=out.at[5, 0], send_sem=relay_sent,
+            recv_sem=out_got.at[5, 0], device_id={"section": 7}, device_id_type=MESH,
         )
 
     def own_copy(lat, slot, member):
@@ -338,7 +352,12 @@
             [real[:, :HALF], imag[:, :HALF], real[:, HALF:] + imag[:, HALF:]], axis=1
         ).astype(BF)
         send_one[lat] = spectrum.reshape(SHT, 2, 2 * C)
-        exchange(send_one.at[lat], recv_one.at[lat], sent.at[lat], got.at[lat])
+        exchange(send_one.at[lat], recv_one.at[lat], sent.at[lat], got.at[lat], 0, FAR)
+        if lat == 1:
+            for each in range(2):
+                exchange(
+                    send_one.at[each], recv_one.at[each], sent.at[each], got.at[each], FAR
+                )
 
     def step(block, carry):
         away = section != block
@@ -462,9 +481,19 @@
                 axis=1,
             ).astype(BF)
 
-            @pl.when(away)
+            detour = jnp.logical_and(block == SECTIONS - 1, section == 2)
+            if lat == 1:
+                detour = False
+
+            @pl.when(jnp.logical_and(away, jnp.logical_not(detour)))
             def _():
                 out_copy(lat, slot, own, block).start()
+
+            if lat == 0:
+
+                @pl.when(detour)
+                def _():
+                    to_relay().start()
 
             @pl.when(jnp.logical_not(away))
             def _():
@@ -511,6 +540,13 @@
         for slot in range(2):
             for lat in range(2):
                 wait_left(lat, slot)
+
+    @pl.when(section == 4)
+    def _():
+        pltpu.make_async_copy(relay, relay, relay_got).wait()
+        copy = from_relay()
+        copy.start()
+        copy.wait_send()
 
     for target in HOME:
 
@@ -552,6 +588,9 @@
             pltpu.VMEM((NLON, 2 * MMAX), BF),
             pltpu.VMEM((8, 2 * NLAT), F32),
             pltpu.SemaphoreType.DMA((11,)),
+            pltpu.VMEM((NLON // 2, 2 * C), BF),
+            pltpu.SemaphoreType.DMA,
+            pltpu.SemaphoreType.DMA,
             pltpu.VMEM((MEMBERS, lats, C // SECTIONS, NLON), BF),
             pltpu.VMEM((SECTIONS, lats, C // SECTIONS, NLON), BF),
             pltpu.VMEM((2, NLON, HALF), F32),

time: 174 us -> 170 us (0.977)
  Pallas kernels: 171 us -> 167 us
    pallas_call x1, Pallas kernels: 171 us -> 167 us  [per_device(): pl.pallas_call(kernel, out_shape=jax.ShapeDtypeStruct((MEMBERS, lats, NLO...]
where the time goes in v6:
time: 170 us
  Pallas kernels  167 us (98%)
  local copies, waits for them, and re-layouts  3.22 us (2%)
    pallas_call x1, Pallas kernels, per_device(): pl.pallas_call(kernel, out_shape=jax.ShapeDtypeStruct((MEMBERS, lats, NLO...  167 us

profile of v6, /device:TPU:1, one launch (start us, length us, event | category | flops | bytes accessed | tf_op | source)
XLA Modules:
  0.0 170.2 jit_solution(9925748750234260573)
XLA Ops:
  0.0 167.0 %shard_map.109 = bf16[6,2,128,384]{3,2,1,0:T(8,128)(2,1)} custom-call(bf16[2,24,256]{2,1,0:T(8,128)(2,1)} %bitcast.15, bf16[6,2,24,256]{3,2,1,0:T(8,128)(2,1)} %bitcast.11, f32[1,192]{1,0:T(1,128)} %gain_first_in.1, f32[1,192]{1,0:T(1,128)} %gain_second_in.1, f32[64,3,2,128]{3,2,1,0:T(2,128)} %bitcast.10, bf16[192,192]{1,0:T(8,128)(2,1)} %bitcast.14, ...), custom_call_target="tpu_custom_call" | custom-call | tf_op jit(solution)/shard_map/pallas_call | solution.py:575
  167.0 3.2 %reshape.3 = bf16[1,6,2,49152]{3,2,1,0:T(2,128)(2,1)} reshape(bf16[6,2,128,384]{3,2,1,0:T(8,128)(2,1)} %shard_map.109) | data formatting | bytes 2359296 | tf_op jit(solution)/shard_map/reshape | solution.py:641
